TPU v7x, 32 devices: a whole 2x2x4 slice. The times are simulated.
32 devices in a mesh: cuts: 4 (over x, core), stem: 8 (over z, y).
Axes of the slice: x: 2, y: 2, z: 4, core: 2. Of those that a mesh axis runs over, the one named last changes fastest.
Arguments:
- stems: bfloat16 [4, 8, 128, 2, 512], P('cuts', 'stem'), may hold values from -6 to 6
- branches: bfloat16 [2, 2, 2, 512, 512], replicated, may hold values from -0.1875 to 0.1875
- closing: bfloat16 [2, 2, 512, 256], replicated, may hold values from -0.09375 to 0.09375
- slice_values: int32 [4, 3], P('cuts'), may hold values from 0 to 1
- mode_perms: int32 [3, 9], replicated, may hold values from 0 to 8, each once within a row
- owner_map: int32 [4], replicated, may hold values from 0 to 3, each once
Outputs:
- open_amplitudes: float32 [8, 4, 2, 64, 128], P('stem', 'cuts')
Inputs may be any that keep to these rules, and one draw needn't show every extreme that they name: `mode_perms`: each row is a permutation of the 9 modes. `owner_map`: a permutation of the owner indices.
All inputs are finite; a program needn't handle non-finite values.
Results may differ from a plain program's by a relative error of at most 0.017.
Values may be sent and summed in bfloat16 or wider, within the bound.
No kernel may reach another device: no remote copies, remote signals or barrier semaphores. Data moves between devices by JAX's collectives and lax.ppermute only.
A program may use at most 64 MiB of HBM per device.

v0:
```python
import jax
import jax.numpy as jnp
from jax import lax
from jax.sharding import PartitionSpec as P


def inverse_order(perm, width):
    column = jnp.arange(width, dtype=jnp.int32)
    result = jnp.zeros((width,), jnp.int32)
    for bit in range(perm.shape[0]):
        moved = jnp.bitwise_and(jnp.right_shift(column, perm[bit]), 1)
        result = result + jnp.left_shift(moved, bit)
    return result


def complex_block(pair):
    real_part = pair[0]
    imag_part = pair[1]
    top = jnp.concatenate([real_part, imag_part], axis=1)
    bottom = jnp.concatenate([-imag_part, real_part], axis=1)
    return jnp.concatenate([top, bottom], axis=0)


def body(stems, branches, closing, slice_values, mode_perms, owner_map):
    groups = lax.axis_size("stem")
    cuts = lax.axis_size("cuts")
    rows = stems.shape[2]
    width = stems.shape[4]
    half = closing.shape[3]
    high = rows // groups
    narrow = width // groups
    piece_width = half // cuts
    chosen = slice_values[0]
    first_pair = jnp.take(branches[0, chosen[0]], inverse_order(mode_perms[0], width), axis=1)
    second_pair = jnp.take(branches[1, chosen[1]], inverse_order(mode_perms[1], width), axis=1)
    last_pair = jnp.take(closing[chosen[2]], inverse_order(mode_perms[2], width), axis=1)
    last_pair = jnp.take(last_pair.reshape(2, width, cuts, piece_width), owner_map, axis=2)
    first_mat = complex_block(first_pair)
    second_mat = complex_block(second_pair)
    real_last = last_pair[0]
    imag_last = last_pair[1]
    upper = jnp.stack([real_last, imag_last], axis=1)
    lower = jnp.stack([-imag_last, real_last], axis=1)
    last_mat = jnp.stack([upper, lower], axis=0)
    state = stems.reshape(rows, 2 * width)
    begun = jnp.dot(state, first_mat, preferred_element_type=jnp.float32).astype(jnp.bfloat16)
    outgoing = jnp.transpose(begun.reshape(high, groups, 2, groups, narrow), (3, 0, 2, 1, 4))
    piece = lax.all_to_all(outgoing, "stem", split_axis=0, concat_axis=0, tiled=True)
    count = piece.shape[1]
    flat = piece.reshape(groups * count, 2 * width)
    out = jnp.dot(flat, second_mat, preferred_element_type=jnp.float32).astype(jnp.bfloat16)
    mixed = out.reshape(groups, count, 2, width)
    mixed = mixed.reshape(rows, 2, width)
    leaving = jnp.transpose(mixed.reshape(high, groups, 2, groups, narrow), (3, 0, 2, 1, 4))
    arrived = lax.all_to_all(leaving, "stem", split_axis=0, concat_axis=0, tiled=True).reshape(
        rows, 2 * width
    )
    block = last_mat
    block = block.reshape(2 * width, 2, lax.axis_size("cuts") * 1, piece_width)
    summed = lax.psum_scatter(
        jnp.einsum("rm,mqbk->bqkr", arrived, block, preferred_element_type=jnp.float32).astype(
            jnp.bfloat16
        ),
        "cuts",
        scatter_dimension=0,
        tiled=True,
    ).astype(jnp.float32)
    return summed.reshape(1, 1, 2, piece_width, rows)


def solution(mesh):
    in_specs = (P("cuts", "stem", None, None, None), P(), P(), P("cuts", None), P(), P())
    out_specs = P("stem", "cuts", None, None, None)
    return jax.shard_map(body, mesh=mesh, in_specs=in_specs, out_specs=out_specs, check_vma=False)
```

profile of v0, /device:TPU:0, one launch (start us, length us, event | category | flops | bytes accessed | tf_op | source)
XLA Modules:
  0.0 143.2 jit_solution(5185854504091047537)
XLA Ops:
  6.5 1.4 fusion.38
  10.5 2.1 %fusion.36 = (s32[1,1]{1,0:T(1,128)}, s32[1,1]{1,0:T(1,128)}, s32[1,1]{1,0:T(1,128)}, s32[1,1]{1,0:T(1,128)}, s32[1,1]{1,0:T(1,128)}, /*index=5*/s32[1,1]{1,0:T(...) fusion(s32[3,9]{1,0:T(4,128)} %param.12), kind=kLoop, calls=%fused_computation.69 | loop fusion | bytes 152 | tf_op jit(solution)/shard_map/slice | solution.py:11
  12.6 5.8 %compare_and_fusion.1 = (pred[512]{0:T(512)(128)(4,1)S(1)}, s32[512]{0:T(512)S(1)}) fusion(s32[]{:T(128)} %bitcast.27, s32[]{:T(128)} %bitcast.26, s32[]{:T(128)} %bitcast.25, s32[]{:T(128)} %bitcast.24, s32[]{:T(128)} %bitcast.23, s32[]{:T(128)} %bitcast.22, s32[]{:T(128)} %bitcast.21, s32[]{:T(128)} %bitcast.20, s32[]{:T(128)} %bitcast.19), kind=kLoop, calls=%fused_computation.56 | loop fusion | flops 20992 | bytes 2596 | tf_op jit(solution)/shard_map/jit(_take)/and | solution.py:34
  19.7 1.7 %constant_dynamic-slice_fusion = (bf16[1,1,2,512,512]{4,3,2,1,0:T(8,128)(2,1)S(1)}, bf16[1,1,2,512,512]{4,3,2,1,0:T(8,128)(2,1)S(1)}) fusion(bf16[2,2,2,512,512]{4,3,2,1,0:T(8,128)(2,1)} %param.9, s32[]{:T(128)S(6)} %select_n.52, s32[]{:T(128)S(6)} %select_n.51), kind=kLoop, calls=%fused_computation.59 | loop fusion | bytes 4194312 | tf_op jit(solution)/shard_map/dynamic_slice | solution.py:35
  21.3 7.5 %copy_bitcast_fusion = (bf16[2,512,512]{2,0,1:T(2,128)(2,1)S(1)}, bf16[2,512,512]{2,0,1:T(2,128)(2,1)}) fusion(bf16[1,1,2,512,512]{4,3,2,1,0:T(8,128)(2,1)S(1)} %get-tuple-element.14, bf16[1,1,2,512,512]{4,3,2,1,0:T(8,128)(2,1)S(1)} %get-tuple-element.15), kind=kLoop, calls=%fused_computation.28 | loop fusion | bytes 4194304 | tf_op jit(solution)/shard_map/squeeze | solution.py:35
  28.9 4.2 %gather_fusion.2 = bf16[512,2,512]{2,1,0:T(2,128)(2,1)S(1)} fusion(bf16[2,512,512]{2,0,1:T(2,128)(2,1)} %get-tuple-element.55, s32[1024]{0:T(1024)S(1)} %pad_clamp_fusion.1), kind=kCustom, calls=%fused_computation.clone | custom fusion | bytes 2099200 | tf_op jit(solution)/shard_map/jit(_take)/gather | solution.py:34
  33.1 2.0 %fusion.26 = bf16[2,512,512]{2,0,1:T(2,128)(2,1)S(1)} fusion(bf16[512,2,512]{2,1,0:T(2,128)(2,1)S(1)} %gather_fusion.2, pred[512]{0:T(512)(128)(4,1)S(1)} %get-tuple-element.12), kind=kLoop, calls=%fused_computation.30 | loop fusion | flops 524288 | bytes 2097664 | tf_op jit(solution)/shard_map/jit(_take)/select_n | solution.py:34
  35.1 1.5 %fusion.35 = (bf16[1,512,512]{2,0,1:T(2,128)(2,1)S(1)}, bf16[1,512,512]{2,0,1:T(2,128)(2,1)S(1)}) fusion(bf16[2,512,512]{2,0,1:T(2,128)(2,1)S(1)} %fusion.26), kind=kLoop, calls=%fused_computation.68 | loop fusion | bytes 2097152 | tf_op jit(solution)/shard_map/slice | solution.py:18
  36.9 0.8 fusion.22
  38.6 1.1 reshape.303
  39.7 7.3 %all-to-all-start = ((bf16[8,2,8192]{2,1,0:T(2,128)(2,1)}), bf16[8,2,8192]{2,1,0:T(2,128)(2,1)S(1)}, u32[]{:S(2)}, u32[]{:S(2)}) async-start(bf16[8,2,8192]{2,1,0:T(2,128)(2,1)} %reshape.303), calls=%async_computation | async-start | bytes 524288 | tf_op jit(solution)/shard_map/all_to_all | solution.py:48
  47.0 0.7 fusion.37
  48.9 5.8 %compare_select_fusion = s32[512,1]{0,1:T(1,128)S(1)} fusion(s32[]{:T(128)} %bitcast.8, s32[]{:T(128)} %bitcast.7, s32[]{:T(128)} %bitcast.6, s32[]{:T(128)} %bitcast.5, s32[]{:T(128)} %bitcast.4, s32[]{:T(128)} %bitcast.3, s32[]{:T(128)} %bitcast.2, s32[]{:T(128)} %bitcast.1, s32[]{:T(128)} %bitcast), kind=kLoop, calls=%fused_computation.46 | loop fusion | flops 19456 | bytes 2084 | tf_op jit(solution)/shard_map/jit(_take)/jit(_where)/select_n | solution.py:36
  54.8 5.8 %compare_and_fusion.2 = pred[512]{0:T(512)(128)(4,1)S(1)} fusion(s32[]{:T(128)} %bitcast.8, s32[]{:T(128)} %bitcast.7, s32[]{:T(128)} %bitcast.6, s32[]{:T(128)} %bitcast.5, s32[]{:T(128)} %bitcast.4, s32[]{:T(128)} %bitcast.3, s32[]{:T(128)} %bitcast.2, s32[]{:T(128)} %bitcast.1, s32[]{:T(128)} %bitcast), kind=kLoop, calls=%fused_computation.57 | loop fusion | flops 20992 | bytes 548 | tf_op jit(solution)/shard_map/jit(_take)/and | solution.py:36
  60.7 5.4 %compare_and_fusion = (pred[512]{0:T(512)(128)(4,1)S(1)}, s32[512]{0:T(512)S(1)}) fusion(s32[]{:T(128)} %bitcast.41, s32[]{:T(128)} %bitcast.40, s32[]{:T(128)} %bitcast.39, s32[]{:T(128)} %bitcast.38, s32[]{:T(128)} %bitcast.37, s32[]{:T(128)} %bitcast.36, s32[]{:T(128)} %bitcast.35, s32[]{:T(128)} %bitcast.34, s32[]{:T(128)} %bitcast.33), kind=kLoop, calls=%fused_computation.55 | loop fusion | flops 20992 | bytes 2596 | tf_op jit(solution)/shard_map/jit(_take)/and | solution.py:35
  66.1 3.6 %gather_fusion.3 = bf16[512,2,512]{2,1,0:T(2,128)(2,1)S(1)} fusion(bf16[2,512,512]{2,0,1:T(2,128)(2,1)S(1)} %get-tuple-element.54, s32[1024]{0:T(1024)S(1)} %pad_clamp_fusion), kind=kCustom, calls=%fused_computation.1.clone | custom fusion | bytes 2099200 | tf_op jit(solution)/shard_map/jit(_take)/gather | solution.py:35
  69.7 2.0 %fusion.27 = bf16[2,512,512]{2,0,1:T(2,128)(2,1)S(1)} fusion(bf16[512,2,512]{2,1,0:T(2,128)(2,1)S(1)} %gather_fusion.3, pred[512]{0:T(512)(128)(4,1)S(1)} %get-tuple-element.8), kind=kLoop, calls=%fused_computation.31 | loop fusion | flops 524288 | bytes 2097664 | tf_op jit(solution)/shard_map/jit(_take)/select_n | solution.py:35
  71.6 1.5 %fusion.34 = (bf16[1,512,512]{2,0,1:T(2,128)(2,1)S(1)}, bf16[1,512,512]{2,0,1:T(2,128)(2,1)S(1)}) fusion(bf16[2,512,512]{2,0,1:T(2,128)(2,1)S(1)} %fusion.27), kind=kLoop, calls=%fused_computation.67 | loop fusion | bytes 2097152 | tf_op jit(solution)/shard_map/slice | solution.py:18
  73.1 0.9 copy.72
  75.3 3.0 %gather_fusion = bf16[512,2,256]{2,1,0:T(2,128)(2,1)} fusion(bf16[2,512,256]{2,0,1:T(2,128)(2,1)S(1)} %bitcast.116, s32[1024]{0:T(1024)S(1)} %pad_clamp_fusion.3), kind=kCustom, calls=%fused_computation.2 | custom fusion | bytes 1050624 | tf_op jit(solution)/shard_map/jit(_take)/gather | solution.py:36
  78.4 1.3 copy.39
  79.7 0.6 gather_fusion.1
  80.5 0.9 slice_bitcast_fusion
  81.3 1.1 fusion.32
  83.2 2.0 %fusion.16 = bf16[128,1024]{1,0:T(8,128)(2,1)S(1)} fusion(bf16[128,1024]{1,0:T(8,128)(2,1)S(1)} %reshape.253, bf16[512,512]{1,0:T(8,128)(2,1)} %bitcast.123, bf16[512,512]{1,0:T(8,128)(2,1)} %get-tuple-element.6, bf16[512,512]{1,0:T(8,128)(2,1)} %get-tuple-element.7), kind=kOutput, calls=%fused_computation.22 | convolution fusion | flops 276955136 | bytes 2097152 | tf_op jit(solution)/shard_map/dot_general | solution.py:51
  86.0 1.1 reshape.305
  87.1 6.0 %all-to-all-start.1 = ((bf16[8,2,8192]{2,1,0:T(2,128)(2,1)}), bf16[8,2,8192]{2,1,0:T(2,128)(2,1)S(1)}, u32[]{:S(2)}, u32[]{:S(2)}) async-start(bf16[8,2,8192]{2,1,0:T(2,128)(2,1)} %reshape.305), calls=%async_computation.1 | async-start | bytes 524288 | tf_op jit(solution)/shard_map/all_to_all | solution.py:55
  93.5 8.1 %all-to-all-done.1 = bf16[8,2,8192]{2,1,0:T(2,128)(2,1)S(1)} async-done(((bf16[8,2,8192]{2,1,0:T(2,128)(2,1)}), bf16[8,2,8192]{2,1,0:T(2,128)(2,1)S(1)}, u32[]{:S(2)}, u32[]{:S(2)}) %all-to-all-start.1) | async-done | bytes 262176 | tf_op jit(solution)/shard_map/all_to_all | solution.py:55
  102.4 1.1 fusion.25
  103.5 0.6 dynamic-slice
  104.2 30.1 %all-reduce.3.cloned.1.call-done = bf16[4,2,64,128]{3,2,0,1:T(8,128)(2,1)} async-done(((bf16[4,2,64,128]{3,2,0,1:T(8,128)(2,1)}), bf16[4,2,64,128]{3,2,0,1:T(8,128)(2,1)}) %all-reduce.3.cloned.1.call-update) | async-done | bytes 131088
  134.3 2.0 %bitcast_convert_fusion = f32[1,1,2,64,128]{4,3,2,1,0:T(8,128)} fusion(bf16[4,2,64,128]{3,2,0,1:T(8,128)(2,1)} %all-reduce.3.cloned.1.call-done, u32[]{:T(128)} %bitcast.55), kind=kLoop, calls=%fused_computation.45 | loop fusion | flops 16384 | bytes 98308 | tf_op jit(solution)/shard_map/reshape | solution.py:68
  (45 shorter events, 4.6 us)
Async XLA Ops:
  6.5 68.2 %copy-start = (bf16[2,2,512,256]{3,2,1,0:T(8,128)(2,1)S(1)}, bf16[2,2,512,256]{3,2,1,0:T(8,128)(2,1)}, u32[]{:S(2)}) copy-start(bf16[2,2,512,256]{3,2,1,0:T(8,128)(2,1)} %param.10) | copy-start | bytes 3145732
  35.1 1.7 %copy-start.3 = (bf16[1,1,128,2,512]{4,3,2,1,0:T(2,128)(2,1)S(1)}, bf16[1,1,128,2,512]{4,3,2,1,0:T(2,128)(2,1)}, u32[]{:S(2)}) copy-start(bf16[1,1,128,2,512]{4,3,2,1,0:T(2,128)(2,1)} %param.8) | copy-start | bytes 786436
  36.9 10.1 %copy-start.4 = (s32[3,9]{1,0:T(4,128)S(1)}, s32[3,9]{1,0:T(4,128)}, u32[]{:S(2)}) copy-start(s32[3,9]{1,0:T(4,128)} %param.12) | copy-start | bytes 328
  36.9 23.7 %copy-start.5 = (s32[4]{0:T(128)S(1)}, s32[4]{0:T(128)}, u32[]{:S(2)}) copy-start(s32[4]{0:T(128)} %param.13) | copy-start | bytes 52
  39.7 42.7 %all-to-all-start = ((bf16[8,2,8192]{2,1,0:T(2,128)(2,1)}), bf16[8,2,8192]{2,1,0:T(2,128)(2,1)S(1)}, u32[]{:S(2)}, u32[]{:S(2)}) async-start(bf16[8,2,8192]{2,1,0:T(2,128)(2,1)} %reshape.303), calls=%async_computation | async-start | bytes 524288 | tf_op jit(solution)/shard_map/all_to_all | solution.py:48
  83.2 10.0 %copy-start.1 = (bf16[512,1,4,64]{0,3,2,1:T(8,128)(2,1)S(1)}, bf16[512,1,4,64]{0,3,2,1:T(8,128)(2,1)}, u32[]{:S(2)}) copy-start(bf16[512,1,4,64]{0,3,2,1:T(8,128)(2,1)} %get-tuple-element.20) | copy-start | bytes 786436
  83.2 10.0 %copy-start.2 = (bf16[512,1,4,64]{0,3,2,1:T(8,128)(2,1)S(1)}, bf16[512,1,4,64]{0,3,2,1:T(8,128)(2,1)}, u32[]{:S(2)}) copy-start(bf16[512,1,4,64]{0,3,2,1:T(8,128)(2,1)} %get-tuple-element.21) | copy-start | bytes 786436
  87.1 14.5 %all-to-all-start.1 = ((bf16[8,2,8192]{2,1,0:T(2,128)(2,1)}), bf16[8,2,8192]{2,1,0:T(2,128)(2,1)S(1)}, u32[]{:S(2)}, u32[]{:S(2)}) async-start(bf16[8,2,8192]{2,1,0:T(2,128)(2,1)} %reshape.305), calls=%async_computation.1 | async-start | bytes 524288 | tf_op jit(solution)/shard_map/all_to_all | solution.py:55
  93.1 41.2 %all-reduce.3.cloned.1.call-start = ((), (), s32[]{:S(2)}) async-start(), calls=%async_computation.2 | async-start | bytes 262144
  93.3 10.2 %copy-start.6 = (u32[32]{0:T(128)S(1)}, u32[32]{0:T(128)}, u32[]{:S(2)}) copy-start(u32[32]{0:T(128)} %constant.62) | copy-start | bytes 388
Sparse Core Ops, SparseCore 0:
  103.6 30.6 all-reduce.2
where the time goes:
time: 144 us; the launch traced here: 143 us
  waiting for transfers between devices  38.2 us (27%)
  local copies, waits for them, and re-layouts  37.8 us (26%)
  other arithmetic  30.4 us (21%)
  between operations  19.5 us (14%)
  starting transfers between devices  13.3 us (9%)
  matrix products  3.87 us (3%)
    unnamed x2, waiting for transfers between devices  30.1 us
    all_to_all x1, waiting for transfers between devices, body(): lax.all_to_all(leaving, 'stem', split_axis=0, concat_axis=0, tiled=True)  8.07 us
    squeeze x1, local copies, waits for them, and re-layouts, body(): branches[1, chosen[1]]  7.53 us
    all_to_all x1, starting transfers between devices, body(): lax.all_to_all(outgoing, 'stem', split_axis=0, concat_axis=0, tiled=True)  7.31 us
    all_to_all x1, starting transfers between devices, body(): lax.all_to_all(leaving, 'stem', split_axis=0, concat_axis=0, tiled=True)  5.99 us
    select_n x2, other arithmetic, body(): jnp.take(closing[chosen[2]], inverse_order(mode_perms[2], width), axis=1)  5.9 us
    and x1, other arithmetic, body(): jnp.take(closing[chosen[2]], inverse_order(mode_perms[2], width), axis=1)  5.84 us
    and x1, other arithmetic, body(): jnp.take(branches[0, chosen[0]], inverse_order(mode_perms[0], width), axi...  5.77 us
  transfers between devices with their start and end apart: 3, of which 2 were waited for; matrix products, arithmetic and copies ran while one was open for 24% of the time, Pallas kernels for 0%

commit v1 on v0

v1 whole, which is shorter than its diff:
```python
import functools

import jax
import jax.numpy as jnp
from jax import lax
from jax.experimental import pallas as pl
from jax.experimental.pallas import tpu as pltpu
from jax.sharding import PartitionSpec as P

BF16 = jnp.bfloat16
F32 = jnp.float32
LANES = 128


def spread(column, modes):
    result = jnp.zeros_like(column)
    for bit, mode in enumerate(modes):
        moved = jnp.bitwise_and(jnp.right_shift(column, bit), 1)
        result = result + jnp.left_shift(moved, mode)
    return result


def stem_kernel(
    groups, values, perms, owners, stems, branches, closing, send,
    first, second, last, orders, amps, flat, pieces, sems,
):
    rows, width = stems.shape[1], stems.shape[2]
    half = last.shape[2]
    narrow = width // groups
    high = rows // groups
    per_tile = LANES // narrow
    copies = (
        pltpu.make_async_copy(branches.at[0, values[0, 0]], first, sems.at[0]),
        pltpu.make_async_copy(branches.at[1, values[0, 1]], second, sems.at[1]),
        pltpu.make_async_copy(closing.at[values[0, 2]], last, sems.at[2]),
    )
    for copy in copies:
        copy.start()
    column = lax.broadcasted_iota(jnp.int32, (1, width), 1)
    entry = lax.broadcasted_iota(jnp.int32, (width, width), 0)
    for step in range(3):
        source = spread(column, [perms[step, bit] for bit in range(perms.shape[1])])
        orders[step] = jnp.where(entry == source, 1.0, 0.0).astype(BF16)

    def absorb(state, step, pair):
        permuted = jnp.dot(state, orders[step], preferred_element_type=F32).astype(BF16)
        by_real = jnp.dot(permuted, pair[0], preferred_element_type=F32)
        by_imag = jnp.dot(permuted, pair[1], preferred_element_type=F32)
        return by_real[:rows] - by_imag[rows:], by_imag[:rows] + by_real[rows:]

    lane = lax.broadcasted_iota(jnp.int32, (high, LANES), 1)

    def relabel(parts):
        for part in range(2):
            for tile in range(width // LANES):
                amps[part, tile] = parts[part][:, tile * LANES : (tile + 1) * LANES]
        for part in range(2):
            for tile in range(width // LANES):
                for start in range(0, groups, per_tile):
                    taken = [
                        amps[part, tile, pl.ds(start + k, high, stride=groups), :] for k in range(per_tile)
                    ]
                    for g in range(per_tile):
                        block = taken[g]
                        for k in range(per_tile):
                            if k != g:
                                moved = pltpu.roll(taken[k], ((k - g) % per_tile) * narrow, 1)
                                block = jnp.where(lane // narrow == k, moved, block)
                        row = part * rows + (tile * per_tile + g) * high
                        at = (start // per_tile) * LANES
                        flat[row : row + high, at : at + LANES] = block.astype(BF16)
        return flat[...]

    state = stems[...].reshape(2 * rows, width)
    copies[0].wait()
    state = relabel(absorb(state, 0, first))
    copies[1].wait()
    state = relabel(absorb(state, 1, second))
    copies[2].wait()
    real, imag = absorb(state, 2, last)
    piece = LANES // 2
    wide = lax.broadcasted_iota(jnp.int32, (rows, LANES), 1) < piece
    for tile in range(half // LANES):
        re = real[:, tile * LANES : (tile + 1) * LANES]
        im = imag[:, tile * LANES : (tile + 1) * LANES]
        pieces[2 * tile] = jnp.where(wide, re, pltpu.roll(im, piece, 1)).astype(BF16)
        pieces[2 * tile + 1] = jnp.where(wide, pltpu.roll(re, piece, 1), im).astype(BF16)
    for owner in range(send.shape[0]):
        send[owner] = pieces[owners[owner]]


def sum_kernel(groups, count, received, total):
    depth, columns = received.shape[0], total.shape[1]
    source = lax.broadcasted_iota(jnp.int32, (depth, columns), 0) % columns
    block = columns // groups
    s, t, x = source // block, (source % block) // count, source % count
    place = (t * groups + s) * count + x
    chosen = jnp.where(place == lax.broadcasted_iota(jnp.int32, (depth, columns), 1), 1.0, 0.0).astype(BF16)
    total[...] = lax.dot_general(
        received[...], chosen, (((0,), (0,)), ((), ())), preferred_element_type=F32
    )


def local_body(stems, branches, closing, slice_values, mode_perms, owner_map):
    groups = lax.axis_size("stem")
    cuts = lax.axis_size("cuts")
    rows, width, half = stems.shape[2], stems.shape[4], closing.shape[3]
    high = rows // groups
    state = jnp.transpose(stems[0, 0], (1, 0, 2))
    vmem, smem = pl.BlockSpec(memory_space=pltpu.VMEM), pl.BlockSpec(memory_space=pltpu.SMEM)
    hbm = pl.BlockSpec(memory_space=pl.ANY)
    send = pl.pallas_call(
        functools.partial(stem_kernel, groups),
        out_shape=jax.ShapeDtypeStruct((cuts, rows, LANES), BF16),
        in_specs=[smem, smem, smem, vmem, hbm, hbm],
        out_specs=vmem,
        scratch_shapes=[
            pltpu.VMEM((2, width, width), BF16),
            pltpu.VMEM((2, width, width), BF16),
            pltpu.VMEM((2, width, half), BF16),
            pltpu.VMEM((3, width, width), BF16),
            pltpu.VMEM((2, width // LANES, rows, LANES), F32),
            pltpu.VMEM((2 * rows, width), BF16),
            pltpu.VMEM((cuts, rows, LANES), BF16),
            pltpu.SemaphoreType.DMA((3,)),
        ],
        name="stem",
    )(slice_values, mode_perms, owner_map, state, branches, closing)
    send = send.reshape(cuts * groups, high, LANES)
    received = lax.all_to_all(send, ("cuts", "stem"), split_axis=0, concat_axis=0, tiled=True)
    total = pl.pallas_call(
        functools.partial(sum_kernel, groups, high // groups),
        out_shape=jax.ShapeDtypeStruct((LANES, rows), F32),
        in_specs=[vmem],
        out_specs=vmem,
        name="total",
    )(received.reshape(cuts * rows, LANES))
    return total.reshape(1, 1, 2, half // cuts, rows)


def absorb(state, perm, pair):
    width = pair.shape[1]
    column = jnp.arange(width, dtype=jnp.int32)
    source = spread(column, [perm[bit] for bit in range(perm.shape[0])])
    order = (column[:, None] == source[None, :]).astype(BF16)
    permuted = jnp.einsum("rpi,ij->prj", state, order, preferred_element_type=F32).astype(BF16)
    product = jnp.einsum("prj,qjk->pqrk", permuted, pair, preferred_element_type=F32)
    return jnp.stack([product[0, 0] - product[1, 1], product[0, 1] + product[1, 0]], axis=1).astype(BF16)


def exchange_body(stems, branches, closing, slice_values, mode_perms, owner_map):
    groups = lax.axis_size("stem")
    cuts = lax.axis_size("cuts")
    rows, width, half = stems.shape[2], stems.shape[4], closing.shape[3]
    high, narrow, piece = rows // groups, width // groups, half // cuts
    chosen = slice_values[0]
    begun = absorb(stems[0, 0], mode_perms[0], branches[0, chosen[0]])
    begun = begun.reshape(high, groups, 2, groups, narrow)
    state = jnp.transpose(begun, (3, 0, 2, 1, 4)).reshape(rows, 2, width)
    mixed = absorb(state, mode_perms[1], branches[1, chosen[1]])
    leaving = jnp.transpose(mixed.reshape(groups, high, 2, groups, narrow), (3, 0, 1, 2, 4))
    arrived = lax.all_to_all(leaving, "stem", split_axis=0, concat_axis=0, tiled=True)
    arrived = jnp.transpose(arrived, (1, 0, 2, 3, 4)).reshape(groups, high, groups, 2, narrow)
    state = jnp.transpose(arrived, (0, 1, 3, 2, 4)).reshape(rows, 2, width)
    final = absorb(state, mode_perms[2], closing[chosen[2]]).reshape(rows, 2, cuts, piece)
    send = jnp.transpose(jnp.take(final, owner_map, axis=2), (2, 1, 3, 0))
    received = lax.all_to_all(send, "cuts", split_axis=0, concat_axis=0, tiled=True)
    total = jnp.sum(received.reshape(cuts, 2, piece, rows).astype(F32), axis=0)
    return total.reshape(1, 1, 2, piece, rows)


def body(*args):
    groups = lax.axis_size("stem")
    rows, width, half = args[0].shape[2], args[0].shape[4], args[2].shape[3]
    high, narrow = rows // groups, width // groups
    local = high % groups == 0 and high % 16 == 0 and LANES % narrow == 0 and groups % (LANES // narrow) == 0
    local = local and 2 * half == LANES * lax.axis_size("cuts") and half % LANES == 0
    return local_body(*args) if local else exchange_body(*args)


def solution(mesh):
    in_specs = (P("cuts", "stem", None, None, None), P(), P(), P("cuts", None), P(), P())
    out_specs = P("stem", "cuts", None, None, None)
    return jax.shard_map(body, mesh=mesh, in_specs=in_specs, out_specs=out_specs, check_vma=False)
```

time: 144 us -> 24.2 us (0.17)
  waiting for transfers between devices: 38.2 us -> 0 us
  local copies, waits for them, and re-layouts: 37.8 us -> 1.67 us
  other arithmetic: 30.4 us -> 0 us
  between operations: 19.5 us -> 0.01 us
  blocking collectives: 0 us -> 15.3 us
  starting transfers between devices: 13.3 us -> 0 us
  Pallas kernels: 0 us -> 7.05 us
  matrix products: 3.87 us -> 0 us
    unnamed x2 -> x0, waiting for transfers between devices: 30.1 us -> none
    and x4 -> x0, other arithmetic: 17 us -> none  [the longest x1 5.84 us: body(): jnp.take(closing[chosen[2]], inverse_order(mode_perms[2], width), axis=1)]
    all_to_all x0 -> x1, blocking collectives: none -> 15.3 us  [local_body(): lax.all_to_all(send, ('cuts', 'stem'), split_axis=0, concat_axis=0, tiled...]
    all_to_all x2 -> x0, starting transfers between devices: 13.3 us -> none  [the longest x1 7.31 us: body(): lax.all_to_all(outgoing, 'stem', split_axis=0, concat_axis=0, tiled=True)]
    gather x5 -> x0, local copies, waits for them, and re-layouts: 12.7 us -> none  [the longest x2 4.34 us: body(): jnp.take(closing[chosen[2]], inverse_order(mode_perms[2], width), axis=1)]
    select_n x6 -> x0, other arithmetic: 9.95 us -> none  [the longest x2 5.9 us: body(): jnp.take(closing[chosen[2]], inverse_order(mode_perms[2], width), axis=1)]
    all_to_all x2 -> x0, waiting for transfers between devices: 8.07 us -> none  [the longest x1 8.07 us: body(): lax.all_to_all(leaving, 'stem', split_axis=0, concat_axis=0, tiled=True)]
    squeeze x1 -> x0, local copies, waits for them, and re-layouts: 7.53 us -> none  [body(): branches[1, chosen[1]]]
  transfers between devices with their start and end apart: 3 -> 0, of which waited for: 2 -> 0; matrix products, arithmetic and copies ran while one was open for 24% -> 0% of each run, Pallas kernels for 0% -> 0%
where the time goes in v1:
time: 24.2 us; the launch traced here: 24 us
  blocking collectives  15.3 us (63%)
  Pallas kernels  7.05 us (29%)
  local copies, waits for them, and re-layouts  1.67 us (7%)
    all_to_all x1, blocking collectives, local_body(): lax.all_to_all(send, ('cuts', 'stem'), split_axis=0, concat_axis=0, tiled...  15.3 us
    pallas_call x1, Pallas kernels, local_body(): pl.pallas_call(functools.partial(stem_kernel, groups), out_shape=jax.Shap...  5.23 us
    pallas_call x1, Pallas kernels, local_body(): pl.pallas_call(functools.partial(sum_kernel, groups, high // groups), out...  1.82 us
    unnamed x1, local copies, waits for them, and re-layouts  1.67 us

profile of v1, /device:TPU:0, one launch (start us, length us, event | category | flops | bytes accessed | tf_op | source)
XLA Modules:
  0.0 24.0 jit_solution(13346780079746139947)
XLA Ops:
  0.0 1.7 %copy.9 = bf16[1,1,128,2,512]{4,2,3,1,0:T(8,128)(2,1)} copy(bf16[1,1,128,2,512]{4,3,2,1,0:T(2,128)(2,1)} %param.6) | data formatting | bytes 524288 | tf_op args[0]
  1.7 5.2 %stem.1 = bf16[4,128,128]{2,1,0:T(8,128)(2,1)} custom-call(s32[1,3]{1,0:T(1,128)} %values.1, s32[3,9]{1,0:T(4,128)} %perms.1, s32[4]{0:T(128)} %owners.1, bf16[2,128,512]{2,1,0:T(8,128)(2,1)} %bitcast.8, bf16[2,2,2,512,512]{4,3,2,1,0:T(8,128)(2,1)} %branches.1, bf16[2,2,512,256]{3,2,1,0:T(8,128)(2,1)} %closing.1), custom_call_target="tpu_custom_call" | custom-call | tf_op jit(solution)/shard_map/stem/pallas_call | solution.py:112
  6.9 15.3 %all_to_all.5 = bf16[32,16,128]{2,1,0:T(8,128)(2,1)} all-to-all(bf16[32,16,128]{2,1,0:T(8,128)(2,1)} %bitcast.9), channel_id=1, replica_groups=mesh['cuts'=4,'stem'=8] {'cuts','stem'}, dimensions={0} | all-to-all | bytes 262144 | tf_op jit(solution)/shard_map/all_to_all | solution.py:130
  22.2 1.8 %total.1 = f32[128,128]{1,0:T(8,128)} custom-call(bf16[512,128]{1,0:T(8,128)(2,1)} %bitcast.10), custom_call_target="tpu_custom_call" | custom-call | tf_op jit(solution)/shard_map/total/pallas_call | solution.py:131

commit v2 on v1

--- a/solution.py
+++ b/solution.py
@@ -22,14 +22,15 @@
 
 def stem_kernel(
     groups, values, perms, owners, stems, branches, closing, send,
-    first, second, last, orders, amps, flat, pieces, sems,
+    begun, first, second, last, orders, amps, flat, pieces, sems, loose,
 ):
-    rows, width = stems.shape[1], stems.shape[2]
+    rows, width = amps.shape[2], first.shape[1]
     half = last.shape[2]
     narrow = width // groups
     high = rows // groups
     per_tile = LANES // narrow
     copies = (
+        pltpu.make_async_copy(stems, begun, sems.at[3]),
         pltpu.make_async_copy(branches.at[0, values[0, 0]], first, sems.at[0]),
         pltpu.make_async_copy(branches.at[1, values[0, 1]], second, sems.at[1]),
         pltpu.make_async_copy(closing.at[values[0, 2]], last, sems.at[2]),
@@ -71,12 +72,19 @@
                         flat[row : row + high, at : at + LANES] = block.astype(BF16)
         return flat[...]
 
-    state = stems[...].reshape(2 * rows, width)
     copies[0].wait()
+    tiles = width // LANES
+    loose[...] = begun[...].astype(F32)
+    for part in range(2):
+        for tile in range(tiles):
+            taken = loose[pl.ds(2 * tile + part, rows, stride=2 * tiles), :]
+            flat[part * rows : (part + 1) * rows, tile * LANES : (tile + 1) * LANES] = taken.astype(BF16)
+    state = flat[...]
+    copies[1].wait()
     state = relabel(absorb(state, 0, first))
-    copies[1].wait()
+    copies[2].wait()
     state = relabel(absorb(state, 1, second))
-    copies[2].wait()
+    copies[3].wait()
     real, imag = absorb(state, 2, last)
     piece = LANES // 2
     wide = lax.broadcasted_iota(jnp.int32, (rows, LANES), 1) < piece
@@ -106,15 +114,16 @@
     cuts = lax.axis_size("cuts")
     rows, width, half = stems.shape[2], stems.shape[4], closing.shape[3]
     high = rows // groups
-    state = jnp.transpose(stems[0, 0], (1, 0, 2))
+    state = jnp.transpose(stems.reshape(rows, 2, width // LANES, LANES), (0, 2, 1, 3)).reshape(-1, LANES)
     vmem, smem = pl.BlockSpec(memory_space=pltpu.VMEM), pl.BlockSpec(memory_space=pltpu.SMEM)
     hbm = pl.BlockSpec(memory_space=pl.ANY)
     send = pl.pallas_call(
         functools.partial(stem_kernel, groups),
-        out_shape=jax.ShapeDtypeStruct((cuts, rows, LANES), BF16),
-        in_specs=[smem, smem, smem, vmem, hbm, hbm],
+        out_shape=pltpu.VMEM((cuts, rows, LANES), BF16),
+        in_specs=[smem, smem, smem, hbm, hbm, hbm],
         out_specs=vmem,
         scratch_shapes=[
+            pltpu.VMEM((2 * rows * width // LANES, LANES), BF16),
             pltpu.VMEM((2, width, width), BF16),
             pltpu.VMEM((2, width, width), BF16),
             pltpu.VMEM((2, width, half), BF16),
@@ -122,7 +131,8 @@
             pltpu.VMEM((2, width // LANES, rows, LANES), F32),
             pltpu.VMEM((2 * rows, width), BF16),
             pltpu.VMEM((cuts, rows, LANES), BF16),
-            pltpu.SemaphoreType.DMA((3,)),
+            pltpu.SemaphoreType.DMA((4,)),
+            pltpu.VMEM((2 * rows * width // LANES, LANES), F32),
         ],
         name="stem",
     )(slice_values, mode_perms, owner_map, state, branches, closing)
@@ -134,7 +144,7 @@
         in_specs=[vmem],
         out_specs=vmem,
         name="total",
-    )(received.reshape(cuts * rows, LANES))
+    )(pltpu.with_memory_space_constraint(received.reshape(cuts * rows, LANES), pltpu.VMEM))
     return total.reshape(1, 1, 2, half // cuts, rows)
 
 

time: 24.2 us -> 20.5 us (0.85)
  Pallas kernels: 7.05 us -> 5.34 us
  local copies, waits for them, and re-layouts: 1.67 us -> 0 us
  blocking collectives: 15.3 us -> 14.9 us
    unnamed x1 -> x0, local copies, waits for them, and re-layouts: 1.67 us -> none
    pallas_call x1, Pallas kernels: 1.82 us -> 0.92 us  [local_body(): pl.pallas_call(functools.partial(sum_kernel, groups, high // groups), out...]
    pallas_call x1, Pallas kernels: 5.23 us -> 4.41 us  [local_body(): pl.pallas_call(functools.partial(stem_kernel, groups), out_shape=pltpu.VM...]
    all_to_all x1, blocking collectives: 15.3 us -> 14.9 us  [local_body(): lax.all_to_all(send, ('cuts', 'stem'), split_axis=0, concat_axis=0, tiled...]
where the time goes in v2:
time: 20.5 us; the launch traced here: 20.3 us
  blocking collectives  14.9 us (73%)
  Pallas kernels  5.34 us (26%)
    all_to_all x1, blocking collectives, local_body(): lax.all_to_all(send, ('cuts', 'stem'), split_axis=0, concat_axis=0, tiled...  14.9 us
    pallas_call x1, Pallas kernels, local_body(): pl.pallas_call(functools.partial(stem_kernel, groups), out_shape=pltpu.VM...  4.41 us
    pallas_call x1, Pallas kernels, local_body(): pl.pallas_call(functools.partial(sum_kernel, groups, high // groups), out...  0.92 us

profile of v2, /device:TPU:0, one launch (start us, length us, event | category | flops | bytes accessed | tf_op | source)
XLA Modules:
  0.0 20.3 jit_solution(15003535773483184102)
XLA Ops:
  0.0 4.4 %stem.1 = bf16[4,128,128]{2,1,0:T(8,128)(2,1)S(1)} custom-call(s32[1,3]{1,0:T(1,128)} %values.1, s32[3,9]{1,0:T(4,128)} %perms.1, s32[4]{0:T(128)} %owners.1, bf16[1024,128]{1,0:T(8,128)(2,1)} %bitcast.10, bf16[2,2,2,512,512]{4,3,2,1,0:T(8,128)(2,1)} %branches.1, bf16[2,2,512,256]{3,2,1,0:T(8,128)(2,1)} %closing.1), custom_call_target="tpu_custom_call" | custom-call | tf_op jit(solution)/shard_map/stem/pallas_call | solution.py:120
  4.4 14.9 %all_to_all.5 = bf16[32,16,128]{2,1,0:T(8,128)(2,1)S(1)} all-to-all(bf16[32,16,128]{2,1,0:T(8,128)(2,1)S(1)} %bitcast.8), channel_id=1, replica_groups=mesh['cuts'=4,'stem'=8] {'cuts','stem'}, dimensions={0} | all-to-all | bytes 262144 | tf_op jit(solution)/shard_map/all_to_all | solution.py:140
  19.4 0.9 %total.1 = f32[128,128]{1,0:T(8,128)} custom-call(bf16[512,128]{1,0:T(8,128)(2,1)S(1)} %bitcast.9), custom_call_target="tpu_custom_call" | custom-call | tf_op jit(solution)/shard_map/total/pallas_call | solution.py:141

commit v3 on v1

v3 whole, which is shorter than its diff:
```python
import functools

import jax
import jax.numpy as jnp
from jax import lax
from jax.experimental import pallas as pl
from jax.experimental.pallas import tpu as pltpu
from jax.sharding import PartitionSpec as P

BF16 = jnp.bfloat16
F32 = jnp.float32
LANES = 128


def spread(column, modes):
    result = jnp.zeros_like(column)
    for bit, mode in enumerate(modes):
        moved = jnp.bitwise_and(jnp.right_shift(column, bit), 1)
        result = result + jnp.left_shift(moved, mode)
    return result


def stem_kernel(
    groups, values_in, perms_in, owners_in, stems, branches, closing, give, keep,
    values, perms, owners, begun, loose, first, second, last, orders, amps, flat, pieces, sems,
):
    rows, width = flat.shape[0] // 2, flat.shape[1]
    half = last.shape[2]
    narrow = width // groups
    high = rows // groups
    tiles = width // LANES
    per_tile = LANES // narrow

    def start(source, target, place):
        copy = pltpu.make_async_copy(source, target, sems.at[place])
        copy.start()
        return copy

    scalars = [
        start(values_in, values, 0),
        start(perms_in, perms, 1),
        start(owners_in, owners, 2),
    ]
    arriving = [start(stems.at[:, l], begun.at[l], 6 + l) for l in range(groups)]
    both = start(branches.at[0], first, 3)
    for copy in scalars:
        copy.wait()
    middle = start(branches.at[1, values[0, 1]], second, 4)
    final = start(closing.at[values[0, 2]], last, 5)

    column = lax.broadcasted_iota(jnp.int32, (1, width), 1)
    deep = 16
    entry = lax.broadcasted_iota(jnp.int32, (deep, width), 0)

    def make_order(step):
        source = spread(column, [perms[step, bit] for bit in range(perms.shape[1])])
        wanted = (jnp.broadcast_to(source, (deep, width)) - entry).astype(jnp.int16)
        for block in range(width // deep):
            orders[step, block * deep : (block + 1) * deep] = jnp.where(
                wanted == jnp.int16(block * deep), jnp.ones((), BF16), jnp.zeros((), BF16)
            )

    def permute(step):
        permuted = jnp.dot(flat[...], orders[step], preferred_element_type=F32).astype(BF16)
        re, im = permuted[:rows], permuted[rows:]
        return jnp.concatenate([jnp.concatenate([re, -im], axis=1), jnp.concatenate([im, re], axis=1)], axis=0)

    def products(state, pair):
        chunk = 2 * LANES
        matrix = pair[...].reshape(2 * width, pair.shape[2])
        for at in range(0, pair.shape[2], chunk):
            product = jnp.dot(state, matrix[:, at : at + chunk], preferred_element_type=F32)
            yield at // LANES, [product[:, k * LANES : (k + 1) * LANES] for k in range(chunk // LANES)]

    lane = lax.broadcasted_iota(jnp.int32, (high, LANES), 1)

    def relabel(part, tile, take):
        for start in range(0, groups, per_tile):
            taken = [take(start + k) for k in range(per_tile)]
            for g in range(per_tile):
                block = taken[g]
                for k in range(per_tile):
                    if k != g:
                        moved = pltpu.roll(taken[k], ((k - g) % per_tile) * narrow, 1)
                        block = jnp.where(lane // narrow == k, moved, block)
                row = part * rows + (tile * per_tile + g) * high
                at = (start // per_tile) * LANES
                flat[row : row + high, at : at + LANES] = block.astype(BF16)

    make_order(0)
    for copy in arriving:
        copy.wait()
    loose[...] = begun[...].astype(F32).reshape(loose.shape)
    for part in range(2):
        for tile in range(tiles):
            taken = loose[pl.ds(2 * tile + part, rows, stride=2 * tiles), :]
            flat[part * rows : (part + 1) * rows, tile * LANES : (tile + 1) * LANES] = taken.astype(BF16)
    state = permute(0)
    make_order(1)
    make_order(2)
    both.wait()
    for at, blocks in products(state, first.at[values[0, 0]]):
        for k, block in enumerate(blocks):
            for part in range(2):
                relabel(part, at + k, lambda l: block[part * rows + l * high : part * rows + (l + 1) * high])
    state = permute(1)
    middle.wait()
    for at, blocks in products(state, second):
        for k, block in enumerate(blocks):
            amps[at + k] = block
            for part in range(2):
                relabel(part, at + k, lambda l: amps[at + k, pl.ds(part * rows + l, high, stride=groups), :])
    state = permute(2)
    final.wait()
    piece = LANES // 2
    wide = lax.broadcasted_iota(jnp.int32, (rows, LANES), 1) < piece
    for at, blocks in products(state, last):
        for k, block in enumerate(blocks):
            re, im = block[:rows], block[rows:]
            pieces[2 * (at + k)] = jnp.where(wide, re, pltpu.roll(im, piece, 1)).astype(BF16)
            pieces[2 * (at + k) + 1] = jnp.where(wide, pltpu.roll(re, piece, 1), im).astype(BF16)
    side = lax.axis_index("cuts") % 2
    for pair in range(give.shape[0]):
        give[pair] = pieces[owners[2 * pair + 1 - side]]
        keep[pair] = pieces[owners[2 * pair + side]]


def pair_kernel(order, high, keep, came, send):
    for place, (pair, group) in enumerate(order):
        rows = slice(group * high, (group + 1) * high)
        total = keep[pair, rows].astype(F32) + came[pair, rows].astype(F32)
        send[place] = total.astype(BF16)


def sum_kernel(order, groups, received, total):
    high, columns = received.shape[1], total.shape[1]
    count = high // groups
    row = lax.broadcasted_iota(jnp.int32, (high, columns), 0)
    first = (row // count) * (groups * count) + row % count
    distance = (lax.broadcasted_iota(jnp.int32, (high, columns), 1) - first).astype(jnp.int16)
    chosen = [
        jnp.where(distance == jnp.int16(group * count), jnp.ones((), BF16), jnp.zeros((), BF16)) for _, group in order
    ]
    total[...] = lax.dot_general(
        received[...].reshape(-1, LANES),
        jnp.concatenate(chosen, axis=0),
        (((0,), (0,)), ((), ())),
        preferred_element_type=F32,
    )


def group_order(pairs, groups):
    order = [(pair, group) for pair in range(pairs) for group in range(groups)]
    return order[::-1]


def local_body(stems, branches, closing, slice_values, mode_perms, owner_map):
    groups = lax.axis_size("stem")
    cuts = lax.axis_size("cuts")
    rows, width, half = stems.shape[2], stems.shape[4], closing.shape[3]
    high = rows // groups
    state = jnp.transpose(stems.reshape(rows, 2, width // LANES, LANES), (0, 2, 1, 3)).reshape(high, groups, -1, LANES)
    vmem, hbm = pl.BlockSpec(memory_space=pltpu.VMEM), pl.BlockSpec(memory_space=pl.ANY)
    half_shape = pltpu.VMEM((cuts // 2, rows, LANES), BF16)
    give, keep = pl.pallas_call(
        functools.partial(stem_kernel, groups),
        out_shape=(half_shape, half_shape),
        in_specs=[hbm] * 6,
        out_specs=(vmem, vmem),
        scratch_shapes=[
            pltpu.SMEM(slice_values.shape, jnp.int32),
            pltpu.SMEM(mode_perms.shape, jnp.int32),
            pltpu.SMEM(owner_map.shape, jnp.int32),
            pltpu.VMEM((groups, high) + state.shape[2:], BF16),
            pltpu.VMEM((2 * rows * width // LANES, LANES), F32),
            pltpu.VMEM(branches.shape[1:], BF16),
            pltpu.VMEM(branches.shape[2:], BF16),
            pltpu.VMEM(closing.shape[1:], BF16),
            pltpu.VMEM((3, width, width), BF16),
            pltpu.VMEM((width // LANES, 2 * rows, LANES), F32),
            pltpu.VMEM((2 * rows, width), BF16),
            pltpu.VMEM((cuts, rows, LANES), BF16),
            pltpu.SemaphoreType.DMA((6 + groups,)),
        ],
        name="stem",
    )(slice_values, mode_perms, owner_map, state, branches, closing)
    came = lax.ppermute(give, "cuts", [(i, i ^ 1) for i in range(cuts)])
    order = group_order(cuts // 2, groups)
    in_vmem = lambda x: pltpu.with_memory_space_constraint(x, pltpu.VMEM)
    send = pl.pallas_call(
        functools.partial(pair_kernel, order, high),
        out_shape=pltpu.VMEM((len(order), high, LANES), BF16),
        in_specs=[vmem, vmem],
        out_specs=vmem,
        name="pair",
    )(in_vmem(keep), in_vmem(came))
    members = [[(2 * pair + side) * groups + group for pair, group in order] for side in range(2)]
    received = lax.all_to_all(
        send, ("cuts", "stem"), split_axis=0, concat_axis=0, axis_index_groups=members, tiled=True
    )
    total = pl.pallas_call(
        functools.partial(sum_kernel, order, groups),
        out_shape=jax.ShapeDtypeStruct((LANES, rows), F32),
        in_specs=[vmem],
        out_specs=vmem,
        name="total",
    )(in_vmem(received))
    return total.reshape(1, 1, 2, half // cuts, rows)


def absorb(state, perm, pair):
    width = pair.shape[1]
    column = jnp.arange(width, dtype=jnp.int32)
    source = spread(column, [perm[bit] for bit in range(perm.shape[0])])
    order = (column[:, None] == source[None, :]).astype(BF16)
    permuted = jnp.einsum("rpi,ij->prj", state, order, preferred_element_type=F32).astype(BF16)
    product = jnp.einsum("prj,qjk->pqrk", permuted, pair, preferred_element_type=F32)
    return jnp.stack([product[0, 0] - product[1, 1], product[0, 1] + product[1, 0]], axis=1).astype(BF16)


def exchange_body(stems, branches, closing, slice_values, mode_perms, owner_map):
    groups = lax.axis_size("stem")
    cuts = lax.axis_size("cuts")
    rows, width, half = stems.shape[2], stems.shape[4], closing.shape[3]
    high, narrow, piece = rows // groups, width // groups, half // cuts
    chosen = slice_values[0]
    begun = absorb(stems[0, 0], mode_perms[0], branches[0, chosen[0]])
    begun = begun.reshape(high, groups, 2, groups, narrow)
    state = jnp.transpose(begun, (3, 0, 2, 1, 4)).reshape(rows, 2, width)
    mixed = absorb(state, mode_perms[1], branches[1, chosen[1]])
    leaving = jnp.transpose(mixed.reshape(groups, high, 2, groups, narrow), (3, 0, 1, 2, 4))
    arrived = lax.all_to_all(leaving, "stem", split_axis=0, concat_axis=0, tiled=True)
    arrived = jnp.transpose(arrived, (1, 0, 2, 3, 4)).reshape(groups, high, groups, 2, narrow)
    state = jnp.transpose(arrived, (0, 1, 3, 2, 4)).reshape(rows, 2, width)
    final = absorb(state, mode_perms[2], closing[chosen[2]]).reshape(rows, 2, cuts, piece)
    send = jnp.transpose(jnp.take(final, owner_map, axis=2), (2, 1, 3, 0))
    received = lax.all_to_all(send, "cuts", split_axis=0, concat_axis=0, tiled=True)
    total = jnp.sum(received.reshape(cuts, 2, piece, rows).astype(F32), axis=0)
    return total.reshape(1, 1, 2, piece, rows)


def body(*args):
    groups = lax.axis_size("stem")
    rows, width, half = args[0].shape[2], args[0].shape[4], args[2].shape[3]
    high, narrow = rows // groups, width // groups
    local = high % groups == 0 and high % 16 == 0 and LANES % narrow == 0 and groups % (LANES // narrow) == 0
    local = local and 2 * half == LANES * lax.axis_size("cuts") and half % LANES == 0 and lax.axis_size("cuts") % 2 == 0
    return local_body(*args) if local else exchange_body(*args)


def solution(mesh):
    in_specs = (P("cuts", "stem", None, None, None), P(), P(), P("cuts", None), P(), P())
    out_specs = P("stem", "cuts", None, None, None)
    return jax.shard_map(body, mesh=mesh, in_specs=in_specs, out_specs=out_specs, check_vma=False)
```

time: 24.2 us -> 18.6 us (0.77)
  blocking collectives: 15.3 us -> 12.1 us
  Pallas kernels: 7.05 us -> 4.77 us
  local copies, waits for them, and re-layouts: 1.67 us -> 0 us
  waiting for transfers between devices: 0 us -> 0.9 us
  starting transfers between devices: 0 us -> 0.56 us
    all_to_all x1, blocking collectives: 15.3 us -> 12.1 us  [local_body(): lax.all_to_all(send, ('cuts', 'stem'), split_axis=0, concat_axis=0, axis_...]
    pallas_call x2 -> x3, Pallas kernels: 7.05 us -> 4.77 us  [the longest x1 3.92 us: local_body(): pl.pallas_call(functools.partial(stem_kernel, groups), out_shape=(half_sh...]
    unnamed x1 -> x0, local copies, waits for them, and re-layouts: 1.67 us -> none
    ppermute x0 -> x1, waiting for transfers between devices: none -> 0.9 us  [local_body(): came = lax.ppermute(give, 'cuts', [(i, i ^ 1) for i in range(cuts)])]
    ppermute x0 -> x1, starting transfers between devices: none -> 0.56 us  [local_body(): came = lax.ppermute(give, 'cuts', [(i, i ^ 1) for i in range(cuts)])]
  transfers between devices with their start and end apart: 0 -> 1, of which waited for: 0 -> 1; matrix products, arithmetic and copies ran while one was open for 0% -> 0% of each run, Pallas kernels for 0% -> 0%
where the time goes in v3:
time: 18.6 us; the launch traced here: 18.4 us
  blocking collectives  12.1 us (65%)
  Pallas kernels  4.77 us (26%)
  waiting for transfers between devices  0.9 us (5%)
  starting transfers between devices  0.56 us (3%)
    all_to_all x1, blocking collectives, local_body(): lax.all_to_all(send, ('cuts', 'stem'), split_axis=0, concat_axis=0, axis_...  12.1 us
    pallas_call x1, Pallas kernels, local_body(): pl.pallas_call(functools.partial(stem_kernel, groups), out_shape=(half_sh...  3.92 us
    ppermute x1, waiting for transfers between devices, local_body(): came = lax.ppermute(give, 'cuts', [(i, i ^ 1) for i in range(cuts)])  0.9 us
    pallas_call x1, Pallas kernels, local_body(): pl.pallas_call(functools.partial(sum_kernel, order, groups), out_shape=ja...  0.83 us
    ppermute x1, starting transfers between devices, local_body(): came = lax.ppermute(give, 'cuts', [(i, i ^ 1) for i in range(cuts)])  0.56 us
  transfers between devices with their start and end apart: 1, of which 1 were waited for; matrix products, arithmetic and copies ran while one was open for 0% of the time, Pallas kernels for 0%

profile of v3, /device:TPU:0, one launch (start us, length us, event | category | flops | bytes accessed | tf_op | source)
XLA Modules:
  0.0 18.4 jit_solution(1272503376266340198)
XLA Ops:
  0.0 3.9 %stem.1 = (bf16[2,128,128]{2,1,0:T(8,128)(2,1)S(1)}, bf16[2,128,128]{2,1,0:T(8,128)(2,1)S(1)}) custom-call(s32[1,3]{1,0:T(1,128)} %values_in.1, s32[3,9]{1,0:T(4,128)} %perms_in.1, s32[4]{0:T(128)} %owners_in.1, bf16[16,8,8,128]{3,2,1,0:T(8,128)(2,1)} %bitcast.6, bf16[2,2,2,512,512]{4,3,2,1,0:T(8,128)(2,1)} %branches.1, bf16[2,2,512,256]{3,2,1,0:T(8,128)(2,1)} %closing.1), custom_call_target="tpu_custom_call" | custom-call | tf_op jit(solution)/shard_map/stem/pallas_call | solution.py:165
  3.9 0.6 %collective-permute-start = (bf16[2,128,128]{2,1,0:T(8,128)(2,1)S(1)}, bf16[2,128,128]{2,1,0:T(8,128)(2,1)S(1)}, u32[]{:S(2)}, u32[]{:S(2)}) collective-permute-start(bf16[2,128,128]{2,1,0:T(8,128)(2,1)S(1)} %get-tuple-element.8), channel_id=1, source_target_pairs={{0,8},{8,0},{16,24},{24,16},{1,9},{9,1},{17,25},{25,17},{2,10},{10... | collective-permute-start | bytes 196616 | tf_op jit(solution)/shard_map/ppermute | solution.py:187
  4.5 0.9 %collective-permute-done.came = bf16[2,128,128]{2,1,0:T(8,128)(2,1)S(1)} collective-permute-done((bf16[2,128,128]{2,1,0:T(8,128)(2,1)S(1)}, bf16[2,128,128]{2,1,0:T(8,128)(2,1)S(1)}, u32[]{:S(2)}, u32[]{:S(2)}) %collective-permute-start) | collective-permute-done | bytes 65568 | tf_op jit(solution)/shard_map/ppermute | solution.py:187
  5.4 12.1 %all_to_all.5.received = bf16[16,16,128]{2,1,0:T(8,128)(2,1)S(1)} all-to-all(bf16[16,16,128]{2,1,0:T(8,128)(2,1)S(1)} %pair.1), channel_id=1, replica_groups={{23,22,21,20,19,18,17,16,7,6,5,4,3,2,1,0},{31,30,29,28,27,26,25,24,15,1..., dimensions={0} | all-to-all | bytes 131072 | tf_op jit(solution)/shard_map/all_to_all | solution.py:198
  17.6 0.8 %total.1 = f32[128,128]{1,0:T(8,128)} custom-call(bf16[16,16,128]{2,1,0:T(8,128)(2,1)S(1)} %all_to_all.5.received), custom_call_target="tpu_custom_call" | custom-call | tf_op jit(solution)/shard_map/total/pallas_call | solution.py:201
  (1 shorter events, 0.0 us)
Async XLA Ops:
  3.9 1.5 %collective-permute-start = (bf16[2,128,128]{2,1,0:T(8,128)(2,1)S(1)}, bf16[2,128,128]{2,1,0:T(8,128)(2,1)S(1)}, u32[]{:S(2)}, u32[]{:S(2)}) collective-permute-start(bf16[2,128,128]{2,1,0:T(8,128)(2,1)S(1)} %get-tuple-element.8), channel_id=1, source_target_pairs={{0,8},{8,0},{16,24},{24,16},{1,9},{9,1},{17,25},{25,17},{2,10},{10... | collective-permute-start | bytes 196616 | tf_op jit(solution)/shard_map/ppermute | solution.py:187

commit v4 on v3

--- a/solution.py
+++ b/solution.py
@@ -22,14 +22,19 @@
 
 def stem_kernel(
     groups, values_in, perms_in, owners_in, stems, branches, closing, give, keep,
-    values, perms, owners, begun, loose, first, second, last, orders, amps, flat, pieces, sems,
+    values, perms, owners, begun, loose, first, second, last, orders, begin, flat, amps, later, pieces, half_way, sems,
 ):
-    rows, width = flat.shape[0] // 2, flat.shape[1]
+    rows, width = begin.shape[0] // 2, begin.shape[1]
     half = last.shape[2]
     narrow = width // groups
     high = rows // groups
+    count = high // groups
     tiles = width // LANES
     per_tile = LANES // narrow
+    chunk = 2 * LANES
+    streams = width // chunk
+    own = groups // streams
+    part_rows = rows // streams
 
     def start(source, target, place):
         copy = pltpu.make_async_copy(source, target, sems.at[place])
@@ -41,12 +46,16 @@
         start(perms_in, perms, 1),
         start(owners_in, owners, 2),
     ]
-    arriving = [start(stems.at[:, l], begun.at[l], 6 + l) for l in range(groups)]
-    both = start(branches.at[0], first, 3)
+    arriving = [start(stems.at[:, l], begun.at[l], 5 + l) for l in range(groups)]
+    variants = branches.shape[1]
+    pairs = [
+        [start(branches.at[0, v, q], first.at[v, q], 5 + groups + q * variants + v) for v in range(variants)]
+        for q in range(2)
+    ]
     for copy in scalars:
         copy.wait()
-    middle = start(branches.at[1, values[0, 1]], second, 4)
-    final = start(closing.at[values[0, 2]], last, 5)
+    middle = start(branches.at[1, values[0, 1]], second, 3)
+    final = start(closing.at[values[0, 2]], last, 4)
 
     column = lax.broadcasted_iota(jnp.int32, (1, width), 1)
     deep = 16
@@ -60,32 +69,50 @@
                 wanted == jnp.int16(block * deep), jnp.ones((), BF16), jnp.zeros((), BF16)
             )
 
-    def permute(step):
-        permuted = jnp.dot(flat[...], orders[step], preferred_element_type=F32).astype(BF16)
-        re, im = permuted[:rows], permuted[rows:]
-        return jnp.concatenate([jnp.concatenate([re, -im], axis=1), jnp.concatenate([im, re], axis=1)], axis=0)
-
-    def products(state, pair):
-        chunk = 2 * LANES
-        matrix = pair[...].reshape(2 * width, pair.shape[2])
-        for at in range(0, pair.shape[2], chunk):
-            product = jnp.dot(state, matrix[:, at : at + chunk], preferred_element_type=F32)
-            yield at // LANES, [product[:, k * LANES : (k + 1) * LANES] for k in range(chunk // LANES)]
-
-    lane = lax.broadcasted_iota(jnp.int32, (high, LANES), 1)
-
-    def relabel(part, tile, take):
-        for start in range(0, groups, per_tile):
-            taken = [take(start + k) for k in range(per_tile)]
-            for g in range(per_tile):
-                block = taken[g]
-                for k in range(per_tile):
-                    if k != g:
-                        moved = pltpu.roll(taken[k], ((k - g) % per_tile) * narrow, 1)
-                        block = jnp.where(lane // narrow == k, moved, block)
-                row = part * rows + (tile * per_tile + g) * high
-                at = (start // per_tile) * LANES
-                flat[row : row + high, at : at + LANES] = block.astype(BF16)
+    def permute(step, state):
+        permuted = jnp.dot(state, orders[step], preferred_element_type=F32).astype(BF16)
+        part = permuted.shape[0] // 2
+        re, im = permuted[:part], permuted[part:]
+        return permuted, jnp.concatenate([-im, re], axis=0)
+
+    def product(factors, pair):
+        state = jnp.concatenate(factors, axis=1)
+        return jnp.dot(state, pair[...].reshape(-1, pair.shape[2]), preferred_element_type=F32)
+
+    def relabel(taken, target, at, row):
+        lane = lax.broadcasted_iota(jnp.int32, taken[0].shape, 1) // narrow
+        blocks = []
+        for g in range(per_tile):
+            block = taken[g]
+            for k in range(per_tile):
+                if k != g:
+                    moved = pltpu.roll(taken[k], ((k - g) % per_tile) * narrow, 1)
+                    block = jnp.where(lane == k, moved, block)
+            blocks.append(block)
+        block = jnp.concatenate(blocks, axis=0).astype(BF16)
+        target[row : row + block.shape[0], at * LANES : (at + 1) * LANES] = block
+
+    def relabel_first(stream, y):
+        for k in range(chunk // LANES):
+            for part in range(2):
+                for at in range(tiles):
+                    taken = [
+                        y[part * rows + l * high : part * rows + (l + 1) * high, k * LANES : (k + 1) * LANES]
+                        for l in range(at * per_tile, (at + 1) * per_tile)
+                    ]
+                    relabel(taken, flat.at[stream], at, part * part_rows + k * per_tile * high)
+
+    def relabel_second(stream, y):
+        for tile in range(tiles):
+            amps[stream, tile] = y[:, tile * LANES : (tile + 1) * LANES]
+        for tile in range(tiles):
+            for part in range(2):
+                for at in range(tiles):
+                    taken = [
+                        amps[stream, tile, pl.ds(part * part_rows + l, own * count, stride=groups), :]
+                        for l in range(at * per_tile, (at + 1) * per_tile)
+                    ]
+                    relabel(taken, later.at[stream], at, part * part_rows + tile * per_tile * own * count)
 
     make_order(0)
     for copy in arriving:
@@ -94,35 +121,48 @@
     for part in range(2):
         for tile in range(tiles):
             taken = loose[pl.ds(2 * tile + part, rows, stride=2 * tiles), :]
-            flat[part * rows : (part + 1) * rows, tile * LANES : (tile + 1) * LANES] = taken.astype(BF16)
-    state = permute(0)
+            begin[part * rows : (part + 1) * rows, tile * LANES : (tile + 1) * LANES] = taken.astype(BF16)
+    factors = permute(0, begin[...])
     make_order(1)
     make_order(2)
-    both.wait()
-    for at, blocks in products(state, first.at[values[0, 0]]):
-        for k, block in enumerate(blocks):
-            for part in range(2):
-                relabel(part, at + k, lambda l: block[part * rows + l * high : part * rows + (l + 1) * high])
-    state = permute(1)
+    chosen = first.at[values[0, 0]]
+    for copy in pairs[0]:
+        copy.wait()
+    for i in range(streams):
+        half_way[i] = jnp.dot(factors[0], chosen[0, :, i * chunk : (i + 1) * chunk], preferred_element_type=F32)
+    for copy in pairs[1]:
+        copy.wait()
+    y = [
+        half_way[i] + jnp.dot(factors[1], chosen[1, :, i * chunk : (i + 1) * chunk], preferred_element_type=F32)
+        for i in range(streams)
+    ]
+    state = []
+    for i in range(streams):
+        relabel_first(i, y[i])
+        state.append(permute(1, flat[i]))
     middle.wait()
-    for at, blocks in products(state, second):
-        for k, block in enumerate(blocks):
-            amps[at + k] = block
-            for part in range(2):
-                relabel(part, at + k, lambda l: amps[at + k, pl.ds(part * rows + l, high, stride=groups), :])
-    state = permute(2)
     final.wait()
+    y = [product(state[i], second) for i in range(streams)]
+    state = []
+    for i in range(streams):
+        relabel_second(i, y[i])
+        state.append(permute(2, later[i]))
     piece = LANES // 2
-    wide = lax.broadcasted_iota(jnp.int32, (rows, LANES), 1) < piece
-    for at, blocks in products(state, last):
-        for k, block in enumerate(blocks):
-            re, im = block[:rows], block[rows:]
-            pieces[2 * (at + k)] = jnp.where(wide, re, pltpu.roll(im, piece, 1)).astype(BF16)
-            pieces[2 * (at + k) + 1] = jnp.where(wide, pltpu.roll(re, piece, 1), im).astype(BF16)
+    wide = lax.broadcasted_iota(jnp.int32, (part_rows, LANES), 1) < piece
+    depth = own * count
+    for i in range(streams):
+        y = product(state[i], last)
+        for tile in range(half // LANES):
+            re = y[:part_rows, tile * LANES : (tile + 1) * LANES]
+            im = y[part_rows:, tile * LANES : (tile + 1) * LANES]
+            for k, block in enumerate(
+                (jnp.where(wide, re, pltpu.roll(im, piece, 1)), jnp.where(wide, pltpu.roll(re, piece, 1), im))
+            ):
+                pieces[2 * tile + k, :, i * depth : (i + 1) * depth] = block.reshape(groups, depth, LANES).astype(BF16)
     side = lax.axis_index("cuts") % 2
     for pair in range(give.shape[0]):
-        give[pair] = pieces[owners[2 * pair + 1 - side]]
-        keep[pair] = pieces[owners[2 * pair + side]]
+        give[pair] = pieces[owners[2 * pair + 1 - side]].reshape(rows, LANES)
+        keep[pair] = pieces[owners[2 * pair + side]].reshape(rows, LANES)
 
 
 def pair_kernel(order, high, keep, came, send):
@@ -161,6 +201,7 @@
     high = rows // groups
     state = jnp.transpose(stems.reshape(rows, 2, width // LANES, LANES), (0, 2, 1, 3)).reshape(high, groups, -1, LANES)
     vmem, hbm = pl.BlockSpec(memory_space=pltpu.VMEM), pl.BlockSpec(memory_space=pl.ANY)
+    streams = width // (2 * LANES)
     half_shape = pltpu.VMEM((cuts // 2, rows, LANES), BF16)
     give, keep = pl.pallas_call(
         functools.partial(stem_kernel, groups),
@@ -177,10 +218,13 @@
             pltpu.VMEM(branches.shape[2:], BF16),
             pltpu.VMEM(closing.shape[1:], BF16),
             pltpu.VMEM((3, width, width), BF16),
-            pltpu.VMEM((width // LANES, 2 * rows, LANES), F32),
             pltpu.VMEM((2 * rows, width), BF16),
-            pltpu.VMEM((cuts, rows, LANES), BF16),
-            pltpu.SemaphoreType.DMA((6 + groups,)),
+            pltpu.VMEM((streams, 2 * rows // streams, width), BF16),
+            pltpu.VMEM((streams, width // LANES, 2 * rows // streams, LANES), F32),
+            pltpu.VMEM((streams, 2 * rows // streams, width), BF16),
+            pltpu.VMEM((cuts, groups, high, LANES), BF16),
+            pltpu.VMEM((streams, 2 * rows, width // streams), F32),
+            pltpu.SemaphoreType.DMA((5 + groups + 2 * branches.shape[1],)),
         ],
         name="stem",
     )(slice_values, mode_perms, owner_map, state, branches, closing)

time: 18.6 us -> 18.2 us (0.978)
  Pallas kernels: 4.77 us -> 4.37 us
    pallas_call x1, Pallas kernels: 3.92 us -> 3.52 us  [local_body(): pl.pallas_call(functools.partial(stem_kernel, groups), out_shape=(half_sh...]
where the time goes in v4:
time: 18.2 us; the launch traced here: 18 us
  blocking collectives  12.1 us (66%)
  Pallas kernels  4.37 us (24%)
  waiting for transfers between devices  0.9 us (5%)
  starting transfers between devices  0.56 us (3%)
    all_to_all x1, blocking collectives, local_body(): lax.all_to_all(send, ('cuts', 'stem'), split_axis=0, concat_axis=0, axis_...  12.1 us
    pallas_call x1, Pallas kernels, local_body(): pl.pallas_call(functools.partial(stem_kernel, groups), out_shape=(half_sh...  3.52 us
    ppermute x1, waiting for transfers between devices, local_body(): came = lax.ppermute(give, 'cuts', [(i, i ^ 1) for i in range(cuts)])  0.9 us
    pallas_call x1, Pallas kernels, local_body(): pl.pallas_call(functools.partial(sum_kernel, order, groups), out_shape=ja...  0.83 us
    ppermute x1, starting transfers between devices, local_body(): came = lax.ppermute(give, 'cuts', [(i, i ^ 1) for i in range(cuts)])  0.56 us
  transfers between devices with their start and end apart: 1, of which 1 were waited for; matrix products, arithmetic and copies ran while one was open for 0% of the time, Pallas kernels for 0%

profile of v4, /device:TPU:0, one launch (start us, length us, event | category | flops | bytes accessed | tf_op | source)
XLA Modules:
  0.0 18.0 jit_solution(17318648388843420271)
XLA Ops:
  0.0 3.5 %stem.1 = (bf16[2,128,128]{2,1,0:T(8,128)(2,1)S(1)}, bf16[2,128,128]{2,1,0:T(8,128)(2,1)S(1)}) custom-call(s32[1,3]{1,0:T(1,128)} %values_in.1, s32[3,9]{1,0:T(4,128)} %perms_in.1, s32[4]{0:T(128)} %owners_in.1, bf16[16,8,8,128]{3,2,1,0:T(8,128)(2,1)} %bitcast.6, bf16[2,2,2,512,512]{4,3,2,1,0:T(8,128)(2,1)} %branches.1, bf16[2,2,512,256]{3,2,1,0:T(8,128)(2,1)} %closing.1), custom_call_target="tpu_custom_call" | custom-call | tf_op jit(solution)/shard_map/stem/pallas_call | solution.py:206
  3.5 0.6 %collective-permute-start = (bf16[2,128,128]{2,1,0:T(8,128)(2,1)S(1)}, bf16[2,128,128]{2,1,0:T(8,128)(2,1)S(1)}, u32[]{:S(2)}, u32[]{:S(2)}) collective-permute-start(bf16[2,128,128]{2,1,0:T(8,128)(2,1)S(1)} %get-tuple-element.8), channel_id=1, source_target_pairs={{0,8},{8,0},{16,24},{24,16},{1,9},{9,1},{17,25},{25,17},{2,10},{10... | collective-permute-start | bytes 196616 | tf_op jit(solution)/shard_map/ppermute | solution.py:231
  4.1 0.9 %collective-permute-done.came = bf16[2,128,128]{2,1,0:T(8,128)(2,1)S(1)} collective-permute-done((bf16[2,128,128]{2,1,0:T(8,128)(2,1)S(1)}, bf16[2,128,128]{2,1,0:T(8,128)(2,1)S(1)}, u32[]{:S(2)}, u32[]{:S(2)}) %collective-permute-start) | collective-permute-done | bytes 65568 | tf_op jit(solution)/shard_map/ppermute | solution.py:231
  5.0 12.1 %all_to_all.5.received = bf16[16,16,128]{2,1,0:T(8,128)(2,1)S(1)} all-to-all(bf16[16,16,128]{2,1,0:T(8,128)(2,1)S(1)} %pair.1), channel_id=1, replica_groups={{23,22,21,20,19,18,17,16,7,6,5,4,3,2,1,0},{31,30,29,28,27,26,25,24,15,1..., dimensions={0} | all-to-all | bytes 131072 | tf_op jit(solution)/shard_map/all_to_all | solution.py:242
  17.2 0.8 %total.1 = f32[128,128]{1,0:T(8,128)} custom-call(bf16[16,16,128]{2,1,0:T(8,128)(2,1)S(1)} %all_to_all.5.received), custom_call_target="tpu_custom_call" | custom-call | tf_op jit(solution)/shard_map/total/pallas_call | solution.py:245
  (1 shorter events, 0.0 us)
Async XLA Ops:
  3.5 1.5 %collective-permute-start = (bf16[2,128,128]{2,1,0:T(8,128)(2,1)S(1)}, bf16[2,128,128]{2,1,0:T(8,128)(2,1)S(1)}, u32[]{:S(2)}, u32[]{:S(2)}) collective-permute-start(bf16[2,128,128]{2,1,0:T(8,128)(2,1)S(1)} %get-tuple-element.8), channel_id=1, source_target_pairs={{0,8},{8,0},{16,24},{24,16},{1,9},{9,1},{17,25},{25,17},{2,10},{10... | collective-permute-start | bytes 196616 | tf_op jit(solution)/shard_map/ppermute | solution.py:231

commit v5 on v4

--- a/solution.py
+++ b/solution.py
@@ -46,27 +46,23 @@
         start(perms_in, perms, 1),
         start(owners_in, owners, 2),
     ]
-    arriving = [start(stems.at[:, l], begun.at[l], 5 + l) for l in range(groups)]
-    variants = branches.shape[1]
-    pairs = [
-        [start(branches.at[0, v, q], first.at[v, q], 5 + groups + q * variants + v) for v in range(variants)]
-        for q in range(2)
-    ]
+    arriving = start(stems, begun, 5)
+    pairs = [start(branches.at[0, :, q], first.at[:, q], 6 + q) for q in range(2)]
     for copy in scalars:
         copy.wait()
     middle = start(branches.at[1, values[0, 1]], second, 3)
     final = start(closing.at[values[0, 2]], last, 4)
 
     column = lax.broadcasted_iota(jnp.int32, (1, width), 1)
-    deep = 16
-    entry = lax.broadcasted_iota(jnp.int32, (deep, width), 0)
+    packed = 16
+    entry = lax.broadcasted_iota(jnp.int32, (packed, width), 0)
 
     def make_order(step):
         source = spread(column, [perms[step, bit] for bit in range(perms.shape[1])])
-        wanted = (jnp.broadcast_to(source, (deep, width)) - entry).astype(jnp.int16)
-        for block in range(width // deep):
-            orders[step, block * deep : (block + 1) * deep] = jnp.where(
-                wanted == jnp.int16(block * deep), jnp.ones((), BF16), jnp.zeros((), BF16)
+        wanted = (jnp.broadcast_to(source, (packed, width)) - entry).astype(jnp.int16)
+        for block in range(width // packed):
+            orders[step, block * packed : (block + 1) * packed] = jnp.where(
+                wanted == jnp.int16(block * packed), jnp.ones((), BF16), jnp.zeros((), BF16)
             )
 
     def permute(step, state):
@@ -115,9 +111,10 @@
                     relabel(taken, later.at[stream], at, part * part_rows + tile * per_tile * own * count)
 
     make_order(0)
-    for copy in arriving:
-        copy.wait()
-    loose[...] = begun[...].astype(F32).reshape(loose.shape)
+    arriving.wait()
+    deep = 2 * tiles * high
+    for l in range(groups):
+        loose[l * deep : (l + 1) * deep] = begun[:, l].astype(F32).reshape(deep, LANES)
     for part in range(2):
         for tile in range(tiles):
             taken = loose[pl.ds(2 * tile + part, rows, stride=2 * tiles), :]
@@ -126,12 +123,10 @@
     make_order(1)
     make_order(2)
     chosen = first.at[values[0, 0]]
-    for copy in pairs[0]:
-        copy.wait()
+    pairs[0].wait()
     for i in range(streams):
         half_way[i] = jnp.dot(factors[0], chosen[0, :, i * chunk : (i + 1) * chunk], preferred_element_type=F32)
-    for copy in pairs[1]:
-        copy.wait()
+    pairs[1].wait()
     y = [
         half_way[i] + jnp.dot(factors[1], chosen[1, :, i * chunk : (i + 1) * chunk], preferred_element_type=F32)
         for i in range(streams)
@@ -212,7 +207,7 @@
             pltpu.SMEM(slice_values.shape, jnp.int32),
             pltpu.SMEM(mode_perms.shape, jnp.int32),
             pltpu.SMEM(owner_map.shape, jnp.int32),
-            pltpu.VMEM((groups, high) + state.shape[2:], BF16),
+            pltpu.VMEM(state.shape, BF16),
             pltpu.VMEM((2 * rows * width // LANES, LANES), F32),
             pltpu.VMEM(branches.shape[1:], BF16),
             pltpu.VMEM(branches.shape[2:], BF16),
@@ -224,7 +219,7 @@
             pltpu.VMEM((streams, 2 * rows // streams, width), BF16),
             pltpu.VMEM((cuts, groups, high, LANES), BF16),
             pltpu.VMEM((streams, 2 * rows, width // streams), F32),
-            pltpu.SemaphoreType.DMA((5 + groups + 2 * branches.shape[1],)),
+            pltpu.SemaphoreType.DMA((8,)),
         ],
         name="stem",
     )(slice_values, mode_perms, owner_map, state, branches, closing)

time: 18.2 us -> 18 us (0.989)
  no operation moved by 1% of the time
where the time goes in v5:
time: 18 us; the launch traced here: 17.9 us
  blocking collectives  12.2 us (68%)
  Pallas kernels  4.24 us (24%)
  waiting for transfers between devices  0.9 us (5%)
  starting transfers between devices  0.55 us (3%)
    all_to_all x1, blocking collectives, local_body(): lax.all_to_all(send, ('cuts', 'stem'), split_axis=0, concat_axis=0, axis_...  12.2 us
    pallas_call x1, Pallas kernels, local_body(): pl.pallas_call(functools.partial(stem_kernel, groups), out_shape=(half_sh...  3.39 us
    ppermute x1, waiting for transfers between devices, local_body(): came = lax.ppermute(give, 'cuts', [(i, i ^ 1) for i in range(cuts)])  0.9 us
    pallas_call x1, Pallas kernels, local_body(): pl.pallas_call(functools.partial(sum_kernel, order, groups), out_shape=ja...  0.83 us
    ppermute x1, starting transfers between devices, local_body(): came = lax.ppermute(give, 'cuts', [(i, i ^ 1) for i in range(cuts)])  0.55 us
  transfers between devices with their start and end apart: 1, of which 1 were waited for; matrix products, arithmetic and copies ran while one was open for 0% of the time, Pallas kernels for 0%

profile of v5, /device:TPU:0, one launch (start us, length us, event | category | flops | bytes accessed | tf_op | source)
XLA Modules:
  0.0 17.9 jit_solution(2101202615608935578)
XLA Ops:
  0.0 3.4 %stem.1 = (bf16[2,128,128]{2,1,0:T(8,128)(2,1)S(1)}, bf16[2,128,128]{2,1,0:T(8,128)(2,1)S(1)}) custom-call(s32[1,3]{1,0:T(1,128)} %values_in.1, s32[3,9]{1,0:T(4,128)} %perms_in.1, s32[4]{0:T(128)} %owners_in.1, bf16[16,8,8,128]{3,2,1,0:T(8,128)(2,1)} %bitcast.6, bf16[2,2,2,512,512]{4,3,2,1,0:T(8,128)(2,1)} %branches.1, bf16[2,2,512,256]{3,2,1,0:T(8,128)(2,1)} %closing.1), custom_call_target="tpu_custom_call" | custom-call | tf_op jit(solution)/shard_map/stem/pallas_call | solution.py:201
  3.4 0.5 %collective-permute-start = (bf16[2,128,128]{2,1,0:T(8,128)(2,1)S(1)}, bf16[2,128,128]{2,1,0:T(8,128)(2,1)S(1)}, u32[]{:S(2)}, u32[]{:S(2)}) collective-permute-start(bf16[2,128,128]{2,1,0:T(8,128)(2,1)S(1)} %get-tuple-element.8), channel_id=1, source_target_pairs={{0,8},{8,0},{16,24},{24,16},{1,9},{9,1},{17,25},{25,17},{2,10},{10... | collective-permute-start | bytes 196616 | tf_op jit(solution)/shard_map/ppermute | solution.py:226
  4.0 0.9 %collective-permute-done.came = bf16[2,128,128]{2,1,0:T(8,128)(2,1)S(1)} collective-permute-done((bf16[2,128,128]{2,1,0:T(8,128)(2,1)S(1)}, bf16[2,128,128]{2,1,0:T(8,128)(2,1)S(1)}, u32[]{:S(2)}, u32[]{:S(2)}) %collective-permute-start) | collective-permute-done | bytes 65568 | tf_op jit(solution)/shard_map/ppermute | solution.py:226
  4.9 12.2 %all_to_all.5.received = bf16[16,16,128]{2,1,0:T(8,128)(2,1)S(1)} all-to-all(bf16[16,16,128]{2,1,0:T(8,128)(2,1)S(1)} %pair.1), channel_id=1, replica_groups={{23,22,21,20,19,18,17,16,7,6,5,4,3,2,1,0},{31,30,29,28,27,26,25,24,15,1..., dimensions={0} | all-to-all | bytes 131072 | tf_op jit(solution)/shard_map/all_to_all | solution.py:237
  17.0 0.8 %total.1 = f32[128,128]{1,0:T(8,128)} custom-call(bf16[16,16,128]{2,1,0:T(8,128)(2,1)S(1)} %all_to_all.5.received), custom_call_target="tpu_custom_call" | custom-call | tf_op jit(solution)/shard_map/total/pallas_call | solution.py:240
  (1 shorter events, 0.0 us)
Async XLA Ops:
  3.4 1.4 %collective-permute-start = (bf16[2,128,128]{2,1,0:T(8,128)(2,1)S(1)}, bf16[2,128,128]{2,1,0:T(8,128)(2,1)S(1)}, u32[]{:S(2)}, u32[]{:S(2)}) collective-permute-start(bf16[2,128,128]{2,1,0:T(8,128)(2,1)S(1)} %get-tuple-element.8), channel_id=1, source_target_pairs={{0,8},{8,0},{16,24},{24,16},{1,9},{9,1},{17,25},{25,17},{2,10},{10... | collective-permute-start | bytes 196616 | tf_op jit(solution)/shard_map/ppermute | solution.py:226

commit v6 on v5

--- a/solution.py
+++ b/solution.py
@@ -21,7 +21,7 @@
 
 
 def stem_kernel(
-    groups, values_in, perms_in, owners_in, stems, branches, closing, give, keep,
+    groups, swapped, values_in, perms_in, owners_in, stems, branches, closing, give, keep,
     values, perms, owners, begun, loose, first, second, last, orders, begin, flat, amps, later, pieces, half_way, sems,
 ):
     rows, width = begin.shape[0] // 2, begin.shape[1]
@@ -154,10 +154,17 @@
                 (jnp.where(wide, re, pltpu.roll(im, piece, 1)), jnp.where(wide, pltpu.roll(re, piece, 1), im))
             ):
                 pieces[2 * tile + k, :, i * depth : (i + 1) * depth] = block.reshape(groups, depth, LANES).astype(BF16)
-    side = lax.axis_index("cuts") % 2
+    mine, group_rows = lax.axis_index("cuts"), rows // groups
+    team = mine % 2
+    for pair, group in swapped:
+        team = jnp.where((mine // 2 == pair) & (lax.axis_index("stem") == group), 1 - team, team)
     for pair in range(give.shape[0]):
-        give[pair] = pieces[owners[2 * pair + 1 - side]].reshape(rows, LANES)
-        keep[pair] = pieces[owners[2 * pair + side]].reshape(rows, LANES)
+        give[pair] = pieces[owners[2 * pair + 1 - team]].reshape(rows, LANES)
+        keep[pair] = pieces[owners[2 * pair + team]].reshape(rows, LANES)
+    for pair, group in swapped:
+        place = slice(group * group_rows, (group + 1) * group_rows)
+        give[pair, place] = pieces[owners[2 * pair + team], group]
+        keep[pair, place] = pieces[owners[2 * pair + 1 - team], group]
 
 
 def pair_kernel(order, high, keep, came, send):
@@ -186,7 +193,8 @@
 
 def group_order(pairs, groups):
     order = [(pair, group) for pair in range(pairs) for group in range(groups)]
-    return order[::-1]
+    order.insert(0, order.pop(-min(3, len(order))))
+    return order
 
 
 def local_body(stems, branches, closing, slice_values, mode_perms, owner_map):
@@ -197,9 +205,10 @@
     state = jnp.transpose(stems.reshape(rows, 2, width // LANES, LANES), (0, 2, 1, 3)).reshape(high, groups, -1, LANES)
     vmem, hbm = pl.BlockSpec(memory_space=pltpu.VMEM), pl.BlockSpec(memory_space=pl.ANY)
     streams = width // (2 * LANES)
+    swapped = [(0, 0)]
     half_shape = pltpu.VMEM((cuts // 2, rows, LANES), BF16)
     give, keep = pl.pallas_call(
-        functools.partial(stem_kernel, groups),
+        functools.partial(stem_kernel, groups, swapped),
         out_shape=(half_shape, half_shape),
         in_specs=[hbm] * 6,
         out_specs=(vmem, vmem),
@@ -233,7 +242,10 @@
         out_specs=vmem,
         name="pair",
     )(in_vmem(keep), in_vmem(came))
-    members = [[(2 * pair + side) * groups + group for pair, group in order] for side in range(2)]
+    members = [
+        [(2 * pair + (team ^ ((pair, group) in swapped))) * groups + group for pair, group in order]
+        for team in range(2)
+    ]
     received = lax.all_to_all(
         send, ("cuts", "stem"), split_axis=0, concat_axis=0, axis_index_groups=members, tiled=True
     )

time: 18 us -> 17.4 us (0.967)
  the two profiles are of different devices: /device:TPU:0 before, /device:TPU:1 now
where the time goes in v6:
time: 17.4 us; the launch traced here: 17.2 us
  blocking collectives  11.7 us (67%)
  Pallas kernels  4.23 us (24%)
  waiting for transfers between devices  1.23 us (7%)
    all_to_all x1, blocking collectives, local_body(): lax.all_to_all(send, ('cuts', 'stem'), split_axis=0, concat_axis=0, axis_...  11.7 us
    pallas_call x1, Pallas kernels, local_body(): pl.pallas_call(functools.partial(stem_kernel, groups, swapped), out_shape...  3.39 us
    ppermute x1, waiting for transfers between devices, local_body(): came = lax.ppermute(give, 'cuts', [(i, i ^ 1) for i in range(cuts)])  1.23 us
    pallas_call x1, Pallas kernels, local_body(): pl.pallas_call(functools.partial(sum_kernel, order, groups), out_shape=ja...  0.83 us
  transfers between devices with their start and end apart: 1, of which 1 were waited for; matrix products, arithmetic and copies ran while one was open for 0% of the time, Pallas kernels for 0%

profile of v6, /device:TPU:1, one launch (start us, length us, event | category | flops | bytes accessed | tf_op | source)
XLA Modules:
  0.0 17.2 jit_solution(4521742486568644088)
XLA Ops:
  0.0 3.4 %stem.1 = (bf16[2,128,128]{2,1,0:T(8,128)(2,1)S(1)}, bf16[2,128,128]{2,1,0:T(8,128)(2,1)S(1)}) custom-call(s32[1,3]{1,0:T(1,128)} %values_in.1, s32[3,9]{1,0:T(4,128)} %perms_in.1, s32[4]{0:T(128)} %owners_in.1, bf16[16,8,8,128]{3,2,1,0:T(8,128)(2,1)} %bitcast.6, bf16[2,2,2,512,512]{4,3,2,1,0:T(8,128)(2,1)} %branches.1, bf16[2,2,512,256]{3,2,1,0:T(8,128)(2,1)} %closing.1), custom_call_target="tpu_custom_call" | custom-call | tf_op jit(solution)/shard_map/stem/pallas_call | solution.py:210
  3.4 0.1 collective-permute-start
  3.5 1.2 %collective-permute-done.came = bf16[2,128,128]{2,1,0:T(8,128)(2,1)S(1)} collective-permute-done((bf16[2,128,128]{2,1,0:T(8,128)(2,1)S(1)}, bf16[2,128,128]{2,1,0:T(8,128)(2,1)S(1)}, u32[]{:S(2)}, u32[]{:S(2)}) %collective-permute-start) | collective-permute-done | bytes 65568 | tf_op jit(solution)/shard_map/ppermute | solution.py:235
  4.7 11.7 %all_to_all.5.received = bf16[16,16,128]{2,1,0:T(8,128)(2,1)S(1)} all-to-all(bf16[16,16,128]{2,1,0:T(8,128)(2,1)S(1)} %pair.1), channel_id=1, replica_groups={{21,8,1,2,3,4,5,6,7,16,17,18,19,20,22,23},{29,0,9,10,11,12,13,14,15,24,..., dimensions={0} | all-to-all | bytes 131072 | tf_op jit(solution)/shard_map/all_to_all | solution.py:249
  16.4 0.8 %total.1 = f32[128,128]{1,0:T(8,128)} custom-call(bf16[16,16,128]{2,1,0:T(8,128)(2,1)S(1)} %all_to_all.5.received), custom_call_target="tpu_custom_call" | custom-call | tf_op jit(solution)/shard_map/total/pallas_call | solution.py:252
  (1 shorter events, 0.0 us)
Async XLA Ops:
  3.4 1.3 %collective-permute-start = (bf16[2,128,128]{2,1,0:T(8,128)(2,1)S(1)}, bf16[2,128,128]{2,1,0:T(8,128)(2,1)S(1)}, u32[]{:S(2)}, u32[]{:S(2)}) collective-permute-start(bf16[2,128,128]{2,1,0:T(8,128)(2,1)S(1)} %get-tuple-element.8), channel_id=1, source_target_pairs={{0,8},{8,0},{16,24},{24,16},{1,9},{9,1},{17,25},{25,17},{2,10},{10... | collective-permute-start | bytes 196616 | tf_op jit(solution)/shard_map/ppermute | solution.py:235

commit v7 on v6

--- a/solution.py
+++ b/solution.py
@@ -174,21 +174,15 @@
         send[place] = total.astype(BF16)
 
 
-def sum_kernel(order, groups, received, total):
-    high, columns = received.shape[1], total.shape[1]
+def sum_kernel(order, groups, received, total, held):
+    high = received.shape[1]
     count = high // groups
-    row = lax.broadcasted_iota(jnp.int32, (high, columns), 0)
-    first = (row // count) * (groups * count) + row % count
-    distance = (lax.broadcasted_iota(jnp.int32, (high, columns), 1) - first).astype(jnp.int16)
-    chosen = [
-        jnp.where(distance == jnp.int16(group * count), jnp.ones((), BF16), jnp.zeros((), BF16)) for _, group in order
-    ]
-    total[...] = lax.dot_general(
-        received[...].reshape(-1, LANES),
-        jnp.concatenate(chosen, axis=0),
-        (((0,), (0,)), ((), ())),
-        preferred_element_type=F32,
-    )
+    for group in range(groups):
+        block = sum(received[at].astype(F32) for at, (_, g) in enumerate(order) if g == group)
+        for t in range(groups):
+            row = t * groups * count + group * count
+            held[row : row + count] = block[t * count : (t + 1) * count]
+    total[...] = held[...].T
 
 
 def group_order(pairs, groups):
@@ -254,6 +248,7 @@
         out_shape=jax.ShapeDtypeStruct((LANES, rows), F32),
         in_specs=[vmem],
         out_specs=vmem,
+        scratch_shapes=[pltpu.VMEM((rows, LANES), F32)],
         name="total",
     )(in_vmem(received))
     return total.reshape(1, 1, 2, half // cuts, rows)

time: 17.4 us -> 17.3 us (level)
  no operation moved by 1% of the time
where the time goes in v7:
time: 17.3 us; the launch traced here: 17.2 us
  blocking collectives  11.7 us (68%)
  Pallas kernels  4.15 us (24%)
  waiting for transfers between devices  1.23 us (7%)
    all_to_all x1, blocking collectives, local_body(): lax.all_to_all(send, ('cuts', 'stem'), split_axis=0, concat_axis=0, axis_...  11.7 us
    pallas_call x1, Pallas kernels, local_body(): pl.pallas_call(functools.partial(stem_kernel, groups, swapped), out_shape...  3.39 us
    ppermute x1, waiting for transfers between devices, local_body(): came = lax.ppermute(give, 'cuts', [(i, i ^ 1) for i in range(cuts)])  1.23 us
    pallas_call x1, Pallas kernels, local_body(): pl.pallas_call(functools.partial(sum_kernel, order, groups), out_shape=ja...  0.74 us
  transfers between devices with their start and end apart: 1, of which 1 were waited for; matrix products, arithmetic and copies ran while one was open for 0% of the time, Pallas kernels for 0%

profile of v7, /device:TPU:1, one launch (start us, length us, event | category | flops | bytes accessed | tf_op | source)
XLA Modules:
  0.0 17.2 jit_solution(6859848190264431014)
XLA Ops:
  0.0 3.4 %stem.1 = (bf16[2,128,128]{2,1,0:T(8,128)(2,1)S(1)}, bf16[2,128,128]{2,1,0:T(8,128)(2,1)S(1)}) custom-call(s32[1,3]{1,0:T(1,128)} %values_in.1, s32[3,9]{1,0:T(4,128)} %perms_in.1, s32[4]{0:T(128)} %owners_in.1, bf16[16,8,8,128]{3,2,1,0:T(8,128)(2,1)} %bitcast.6, bf16[2,2,2,512,512]{4,3,2,1,0:T(8,128)(2,1)} %branches.1, bf16[2,2,512,256]{3,2,1,0:T(8,128)(2,1)} %closing.1), custom_call_target="tpu_custom_call" | custom-call | tf_op jit(solution)/shard_map/stem/pallas_call | solution.py:204
  3.4 0.1 collective-permute-start
  3.5 1.2 %collective-permute-done.came = bf16[2,128,128]{2,1,0:T(8,128)(2,1)S(1)} collective-permute-done((bf16[2,128,128]{2,1,0:T(8,128)(2,1)S(1)}, bf16[2,128,128]{2,1,0:T(8,128)(2,1)S(1)}, u32[]{:S(2)}, u32[]{:S(2)}) %collective-permute-start) | collective-permute-done | bytes 65568 | tf_op jit(solution)/shard_map/ppermute | solution.py:229
  4.7 11.7 %all_to_all.5.received = bf16[16,16,128]{2,1,0:T(8,128)(2,1)S(1)} all-to-all(bf16[16,16,128]{2,1,0:T(8,128)(2,1)S(1)} %pair.1), channel_id=1, replica_groups={{21,8,1,2,3,4,5,6,7,16,17,18,19,20,22,23},{29,0,9,10,11,12,13,14,15,24,..., dimensions={0} | all-to-all | bytes 131072 | tf_op jit(solution)/shard_map/all_to_all | solution.py:243
  16.4 0.7 %total.1 = f32[128,128]{1,0:T(8,128)} custom-call(bf16[16,16,128]{2,1,0:T(8,128)(2,1)S(1)} %all_to_all.5.received), custom_call_target="tpu_custom_call" | custom-call | tf_op jit(solution)/shard_map/total/pallas_call | solution.py:246
  (1 shorter events, 0.0 us)
Async XLA Ops:
  3.4 1.3 %collective-permute-start = (bf16[2,128,128]{2,1,0:T(8,128)(2,1)S(1)}, bf16[2,128,128]{2,1,0:T(8,128)(2,1)S(1)}, u32[]{:S(2)}, u32[]{:S(2)}) collective-permute-start(bf16[2,128,128]{2,1,0:T(8,128)(2,1)S(1)} %get-tuple-element.8), channel_id=1, source_target_pairs={{0,8},{8,0},{16,24},{24,16},{1,9},{9,1},{17,25},{25,17},{2,10},{10... | collective-permute-start | bytes 196616 | tf_op jit(solution)/shard_map/ppermute | solution.py:229

commit v8 on v7

--- a/solution.py
+++ b/solution.py
@@ -36,9 +36,9 @@
     own = groups // streams
     part_rows = rows // streams
 
-    def start(source, target, place):
+    def start(source, target, place, priority=0):
         copy = pltpu.make_async_copy(source, target, sems.at[place])
-        copy.start()
+        copy.start(priority=priority)
         return copy
 
     scalars = [
@@ -46,12 +46,12 @@
         start(perms_in, perms, 1),
         start(owners_in, owners, 2),
     ]
-    arriving = start(stems, begun, 5)
-    pairs = [start(branches.at[0, :, q], first.at[:, q], 6 + q) for q in range(2)]
+    arriving = start(stems, begun, 5, 0)
+    pairs = [start(branches.at[0, :, q], first.at[:, q], 6 + q, (0, 0)[q]) for q in range(2)]
     for copy in scalars:
         copy.wait()
-    middle = start(branches.at[1, values[0, 1]], second, 3)
-    final = start(closing.at[values[0, 2]], last, 4)
+    middle = start(branches.at[1, values[0, 1]], second, 3, 1)
+    final = start(closing.at[values[0, 2]], last, 4, 1)
 
     column = lax.broadcasted_iota(jnp.int32, (1, width), 1)
     packed = 16

time: 17.3 us -> 17.3 us (level)
  no operation moved by 1% of the time
where the time goes in v8:
time: 17.3 us; the launch traced here: 17.2 us
  blocking collectives  11.7 us (68%)
  Pallas kernels  4.15 us (24%)
  waiting for transfers between devices  1.23 us (7%)
    all_to_all x1, blocking collectives, local_body(): lax.all_to_all(send, ('cuts', 'stem'), split_axis=0, concat_axis=0, axis_...  11.7 us
    pallas_call x1, Pallas kernels, local_body(): pl.pallas_call(functools.partial(stem_kernel, groups, swapped), out_shape...  3.39 us
    ppermute x1, waiting for transfers between devices, local_body(): came = lax.ppermute(give, 'cuts', [(i, i ^ 1) for i in range(cuts)])  1.23 us
    pallas_call x1, Pallas kernels, local_body(): pl.pallas_call(functools.partial(sum_kernel, order, groups), out_shape=ja...  0.74 us
  transfers between devices with their start and end apart: 1, of which 1 were waited for; matrix products, arithmetic and copies ran while one was open for 0% of the time, Pallas kernels for 0%

profile of v8, /device:TPU:1, one launch (start us, length us, event | category | flops | bytes accessed | tf_op | source)
XLA Modules:
  0.0 17.2 jit_solution(8807641763021511915)
XLA Ops:
  0.0 3.4 %stem.1 = (bf16[2,128,128]{2,1,0:T(8,128)(2,1)S(1)}, bf16[2,128,128]{2,1,0:T(8,128)(2,1)S(1)}) custom-call(s32[1,3]{1,0:T(1,128)} %values_in.1, s32[3,9]{1,0:T(4,128)} %perms_in.1, s32[4]{0:T(128)} %owners_in.1, bf16[16,8,8,128]{3,2,1,0:T(8,128)(2,1)} %bitcast.6, bf16[2,2,2,512,512]{4,3,2,1,0:T(8,128)(2,1)} %branches.1, bf16[2,2,512,256]{3,2,1,0:T(8,128)(2,1)} %closing.1), custom_call_target="tpu_custom_call" | custom-call | tf_op jit(solution)/shard_map/stem/pallas_call | solution.py:204
  3.4 0.1 collective-permute-start
  3.5 1.2 %collective-permute-done.came = bf16[2,128,128]{2,1,0:T(8,128)(2,1)S(1)} collective-permute-done((bf16[2,128,128]{2,1,0:T(8,128)(2,1)S(1)}, bf16[2,128,128]{2,1,0:T(8,128)(2,1)S(1)}, u32[]{:S(2)}, u32[]{:S(2)}) %collective-permute-start) | collective-permute-done | bytes 65568 | tf_op jit(solution)/shard_map/ppermute | solution.py:229
  4.7 11.7 %all_to_all.5.received = bf16[16,16,128]{2,1,0:T(8,128)(2,1)S(1)} all-to-all(bf16[16,16,128]{2,1,0:T(8,128)(2,1)S(1)} %pair.1), channel_id=1, replica_groups={{21,8,1,2,3,4,5,6,7,16,17,18,19,20,22,23},{29,0,9,10,11,12,13,14,15,24,..., dimensions={0} | all-to-all | bytes 131072 | tf_op jit(solution)/shard_map/all_to_all | solution.py:243
  16.4 0.7 %total.1 = f32[128,128]{1,0:T(8,128)} custom-call(bf16[16,16,128]{2,1,0:T(8,128)(2,1)S(1)} %all_to_all.5.received), custom_call_target="tpu_custom_call" | custom-call | tf_op jit(solution)/shard_map/total/pallas_call | solution.py:246
  (1 shorter events, 0.0 us)
Async XLA Ops:
  3.4 1.3 %collective-permute-start = (bf16[2,128,128]{2,1,0:T(8,128)(2,1)S(1)}, bf16[2,128,128]{2,1,0:T(8,128)(2,1)S(1)}, u32[]{:S(2)}, u32[]{:S(2)}) collective-permute-start(bf16[2,128,128]{2,1,0:T(8,128)(2,1)S(1)} %get-tuple-element.8), channel_id=1, source_target_pairs={{0,8},{8,0},{16,24},{24,16},{1,9},{9,1},{17,25},{25,17},{2,10},{10... | collective-permute-start | bytes 196616 | tf_op jit(solution)/shard_map/ppermute | solution.py:229
